TPU v7x, 32 devices: a whole 2x2x4 slice. The times are simulated.
32 devices in a mesh: space: 32 (over z, y, x, core).
Axes of the slice: x: 2, y: 2, z: 4, core: 2. Of those that a mesh axis runs over, the one named last changes fastest.
Arguments:
- coords: float32 [512, 3, 128], P('space'), may hold values from -3 to 3
- force: float32 [512, 3, 128], P('space'), may hold values from -12 to 12
- restraint: float32 [512, 128], P('space'), may hold values from 0.25 to 4
- neighbors: int32 [512, 32], P('space'), may hold values from 0 to 511, as said below
- mask: int32 [512, 32], P('space'), may hold values from 0 to 1, as said below
Outputs:
- solution_field: float32 [512, 3, 128], P('space')
- residual: float32 [512, 3, 128], P('space')
Inputs may be any that keep to these rules, and one draw needn't show every extreme that they name: `neighbors`: for every block b, the live entries name distinct blocks c with |c - b| <= 15; b itself is always live; if b lists c live then c lists b live; entries with mask 0 name b itself. `mask`: marks the live entries of neighbors.
All inputs are finite; a program needn't handle non-finite values.
Results may differ from a plain program's by a relative error of at most 0.0003.
Values sent between devices are 32-bit elements; how exact they have to be, the bound alone decides.
No kernel may reach another device: no remote copies, remote signals or barrier semaphores. Data moves between devices by JAX's collectives and lax.ppermute only.
A program may use at most 64 MiB of HBM per device.

v0:
```python
import jax
import jax.numpy as jnp
from jax import lax
from jax.sharding import PartitionSpec as P

ITERS = 2


def with_halo(cells, sides, width):
    for axis, dim in sides:
        count = lax.axis_size(axis)
        ends = count - 1
        head = lax.slice_in_dim(cells, 0, width, axis=dim)
        tail = lax.slice_in_dim(cells, cells.shape[dim] - width, cells.shape[dim], axis=dim)
        cells = jnp.concatenate(
            [
                lax.ppermute(tail, axis, [(i, (i + 1) % count) for i in range(ends)]),
                cells,
                lax.ppermute(head, axis, [((i + 1) % count, i) for i in range(ends)]),
            ],
            axis=dim,
        )
    return cells


def block_product(own_coords, own_values, own_spring, far_coords, far_values, live_flags):
    offset = far_coords[:, :, None, :] - own_coords[None, :, :, None]
    squared = jnp.sum(offset * offset, axis=1)
    soften = 1.0 + squared
    weight = live_flags[:, None, None] / (own_coords.shape[-1] * soften * soften)
    motion = jnp.sum(offset * (own_values[None, :, :, None] - far_values[:, :, None, :]), axis=1)
    strength = weight * motion
    pulled = jnp.sum(strength[:, None, :, :] * offset, axis=(0, 3))
    return own_spring[None, :] * own_values + pulled


def per_device(coords, force, restraint, neighbors, mask):
    blocks = coords.shape[0]
    margin = min(blocks, (neighbors.shape[1] - 1) // 2)
    live_mask = mask.astype(jnp.float32)
    near_index = neighbors - (lax.axis_index("space") * blocks - margin)
    coord_table = with_halo(coords, (("space", 0),), margin)

    def spread(vector):
        return with_halo(vector, (("space", 0),), margin)

    def operate(vector):
        value_table = spread(vector)

        def one_block(packed):
            own_coords, own_values, own_spring, near_rows, live_flags = packed
            return block_product(
                own_coords,
                own_values,
                own_spring,
                coord_table[near_rows],
                value_table[near_rows],
                live_flags,
            )

        return lax.map(one_block, (coords, vector, restraint, near_index, live_mask))

    def two_sums(residual, image):
        return lax.psum((jnp.sum(residual * residual), jnp.sum(residual * image)), "space")

    solution = jnp.zeros_like(force)
    residual = force
    image = operate(residual)
    norm_now, product = two_sums(residual, image)
    step_size = norm_now / product
    direction = residual
    along = image
    for iteration in range(ITERS):
        solution = solution + step_size * direction
        residual = residual - step_size * along
        if iteration + 1 < ITERS:
            image = operate(residual)
            norm_next, product = two_sums(residual, image)
            momentum = norm_next / norm_now
            step_size = norm_next / (product - momentum * norm_next / step_size)
            direction = residual + momentum * direction
            along = image + momentum * along
            norm_now = norm_next
    return (solution, residual)


def solution(mesh):
    in_specs = (
        P("space", None, None),
        P("space", None, None),
        P("space", None),
        P("space", None),
        P("space", None),
    )
    out_specs = (P("space", None, None), P("space", None, None))
    return jax.shard_map(
        per_device, mesh=mesh, in_specs=in_specs, out_specs=out_specs, check_vma=False
    )
```

profile of v0, /device:TPU:0, one launch (start us, length us, event | category | flops | bytes accessed | tf_op | source)
XLA Modules:
  0.0 285.3 jit_solution(1970524849101358119)
XLA Ops:
  1.4 2.4 collective-permute-start.2
  5.9 5.1 %collective-permute-start = (f32[15,3,128]{2,1,0:T(4,128)S(1)}, f32[15,3,128]{2,1,0:T(4,128)S(1)}, u32[]{:S(2)}, u32[]{:S(2)}) collective-permute-start(f32[15,3,128]{2,1,0:T(4,128)S(1)} %get-tuple-element.205), channel_id=1, source_target_pairs={{0,1},{1,2},{2,3},{3,4},{4,5},{5,6},{6,7},{7,8},{8,9},{9,10},{10,1... | collective-permute-start | bytes 69128 | tf_op jit(solution)/shard_map/ppermute | solution.py:17
  15.9 82.4 %while.20 = (s32[]{:T(128)}, f32[16,3,128]{2,1,0:T(4,128)S(1)}, f32[16,128]{1,0:T(8,128)}, f32[16,3,128]{2,1,0:T(4,128)S(1)}, f32[16,32]{1,0:T(8,128)S(1)}, /*in...) while((s32[]{:T(128)}, f32[16,3,128]{2,1,0:T(4,128)S(1)}, ...), condition=%wide.region_6.7_spmd, body=%wide.region_2.0_spmd.sunk | while | flops 15730146 | bytes 12952185 | solution.py:61
  22.4 1.8 fusion.38
  27.5 1.8 fusion.38
  37.8 1.8 fusion.38
  48.1 1.8 fusion.38
  53.2 1.8 fusion.38
  63.5 1.8 fusion.38
  68.7 1.8 fusion.38
  73.8 1.8 fusion.38
  84.1 1.8 fusion.38
  89.3 1.8 fusion.38
  94.4 1.8 fusion.38
  98.9 45.8 %all-reduce.1 = (f32[]{:T(128)}, f32[]{:T(128)}) all-reduce(f32[]{:T(128)} %multiply_reduce_fusion.3, f32[]{:T(128)} %multiply_reduce_fusion), channel_id=1, replica_groups=mesh['space'=32] {'space'}, use_global_device_ids=true, to_apply=%region_1.2 | all-reduce | flops 2 | bytes 16 | tf_op jit(solution)/shard_map/psum | solution.py:64
  148.8 4.3 %collective-permute-done.5 = f32[15,3,128]{2,0,1:T(8,128)S(1)} collective-permute-done((f32[15,3,128]{2,0,1:T(8,128)S(1)}, f32[15,3,128]{2,0,1:T(8,128)S(1)}, u32[]{:S(2)}, u32[]{:S(2)}) %collective-permute-start.5) | collective-permute-done | bytes 23072 | tf_op jit(solution)/shard_map/ppermute | solution.py:19
  153.1 83.9 %while.21 = (s32[]{:T(128)}, f32[16,3,128]{2,0,1:T(8,128)S(1)}, f32[16,128]{1,0:T(8,128)}, f32[16,3,128]{2,0,1:T(8,128)S(1)}, f32[16,32]{1,0:T(8,128)S(1)}, /*in...) while((s32[]{:T(128)}, f32[16,3,128]{2,0,1:T(8,128)S(1)}, ...), condition=%wide.region_15.16_spmd, body=%wide.region_11.15_spmd.sunk | while | flops 15730146 | bytes 12959877 | solution.py:61
  164.9 1.8 fusion.45
  175.4 1.8 fusion.45
  191.2 1.8 fusion.45
  206.9 1.8 fusion.45
  222.6 1.8 fusion.45
  227.9 1.8 fusion.45
  237.7 42.6 %all-reduce = (f32[]{:T(128)}, f32[]{:T(128)}) all-reduce(f32[]{:T(128)} %get-tuple-element.157, f32[]{:T(128)} %get-tuple-element.156), channel_id=1, replica_groups=mesh['space'=32] {'space'}, use_global_device_ids=true, to_apply=%region_10.11 | all-reduce | flops 2 | bytes 16 | tf_op jit(solution)/shard_map/psum | solution.py:64
  (414 shorter events, 145.9 us)
Async XLA Ops:
  1.4 14.4 %collective-permute-start.2 = (f32[15,3,128]{2,1,0:T(4,128)S(1)}, f32[15,3,128]{2,1,0:T(4,128)S(1)}, u32[]{:S(2)}, u32[]{:S(2)}) collective-permute-start(f32[15,3,128]{2,1,0:T(4,128)S(1)} %get-tuple-element.202), channel_id=1, source_target_pairs={{0,1},{1,2},{2,3},{3,4},{4,5},{5,6},{6,7},{7,8},{8,9},{9,10},{10,1... | collective-permute-start | bytes 69128 | tf_op jit(solution)/shard_map/ppermute | solution.py:17
  3.8 12.1 %collective-permute-start.3 = (f32[15,3,128]{2,1,0:T(4,128)S(1)}, f32[15,3,128]{2,1,0:T(4,128)S(1)}, u32[]{:S(2)}, u32[]{:S(2)}) collective-permute-start(f32[15,3,128]{2,1,0:T(4,128)S(1)} %get-tuple-element.203), channel_id=1, source_target_pairs={{1,0},{2,1},{3,2},{4,3},{5,4},{6,5},{7,6},{8,7},{9,8},{10,9},{11,1... | collective-permute-start | bytes 69128 | tf_op jit(solution)/shard_map/ppermute | solution.py:19
  5.9 9.2 %collective-permute-start = (f32[15,3,128]{2,1,0:T(4,128)S(1)}, f32[15,3,128]{2,1,0:T(4,128)S(1)}, u32[]{:S(2)}, u32[]{:S(2)}) collective-permute-start(f32[15,3,128]{2,1,0:T(4,128)S(1)} %get-tuple-element.205), channel_id=1, source_target_pairs={{0,1},{1,2},{2,3},{3,4},{4,5},{5,6},{6,7},{7,8},{8,9},{9,10},{10,1... | collective-permute-start | bytes 69128 | tf_op jit(solution)/shard_map/ppermute | solution.py:17
  11.0 4.9 %collective-permute-start.1 = (f32[15,3,128]{2,1,0:T(4,128)S(1)}, f32[15,3,128]{2,1,0:T(4,128)S(1)}, u32[]{:S(2)}, u32[]{:S(2)}) collective-permute-start(f32[15,3,128]{2,1,0:T(4,128)S(1)} %get-tuple-element.204), channel_id=1, source_target_pairs={{1,0},{2,1},{3,2},{4,3},{5,4},{6,5},{7,6},{8,7},{9,8},{10,9},{11,1... | collective-permute-start | bytes 69128 | tf_op jit(solution)/shard_map/ppermute | solution.py:19
  15.9 82.4 %copy-start = (f32[16,3,128]{2,0,1:T(8,128)S(1)}, f32[16,3,128]{2,0,1:T(8,128)}, u32[]{:S(2)}) copy-start(f32[16,3,128]{2,0,1:T(8,128)} %param.10) | copy-start | bytes 73732
  146.2 2.6 collective-permute-start.4
  147.5 5.6 %collective-permute-start.5 = (f32[15,3,128]{2,0,1:T(8,128)S(1)}, f32[15,3,128]{2,0,1:T(8,128)S(1)}, u32[]{:S(2)}, u32[]{:S(2)}) collective-permute-start(f32[15,3,128]{2,0,1:T(8,128)S(1)} %get-tuple-element.209), channel_id=1, source_target_pairs={{1,0},{2,1},{3,2},{4,3},{5,4},{6,5},{7,6},{8,7},{9,8},{10,9},{11,1... | collective-permute-start | bytes 69128 | tf_op jit(solution)/shard_map/ppermute | solution.py:19
where the time goes:
time: 287 us; the launch traced here: 285 us
  other arithmetic  106 us (37%)
  blocking collectives  88.4 us (31%)
  local copies, waits for them, and re-layouts  65.1 us (23%)
  starting transfers between devices  12.7 us (4%)
  between operations  6.58 us (2%)
  waiting for transfers between devices  4.29 us (1%)
    psum x2, blocking collectives, two_sums(): lax.psum((jnp.sum(residual * residual), jnp.sum(residual * image)), 'space')  88.4 us
    reduce_sum x32, other arithmetic, block_product(): squared = jnp.sum(offset * offset, axis=1)  57.7 us
    reduce_sum x32, other arithmetic, block_product(): pulled = jnp.sum(strength[:, None, :, :] * offset, axis=(0, 3))  27.2 us
    mul x32, local copies, waits for them, and re-layouts, block_product(): return own_spring[None, :] * own_values + pulled  22.3 us
    gather x32, local copies, waits for them, and re-layouts, one_block(): coord_table[near_rows]  19.5 us
    gather x32, local copies, waits for them, and re-layouts, one_block(): value_table[near_rows]  19.5 us
    mul x32, other arithmetic, block_product(): strength = weight * motion  15.7 us
    ppermute x3, starting transfers between devices, with_halo(): lax.ppermute(tail, axis, [(i, (i + 1) % count) for i in range(ends)])  8.82 us
  transfers between devices with their start and end apart: 6, of which 1 were waited for; matrix products, arithmetic and copies ran while one was open for 2% of the time, Pallas kernels for 0%

commit v1 on v0

v1 whole, which is shorter than its diff:
```python
import functools
import jax
import jax.numpy as jnp
from jax import lax
from jax.experimental import pallas as pl
from jax.experimental.pallas import tpu as pltpu
from jax.sharding import PartitionSpec as P

F32 = jnp.float32
BF16 = jnp.bfloat16
DEAD = 2.0 ** 100
FEATS = 32


def vmem():
    return pl.BlockSpec(memory_space=pltpu.VMEM)


def split3(x):
    h = x.astype(BF16).astype(F32)
    rest = x - h
    m = rest.astype(BF16).astype(F32)
    return h, m, (rest - m).astype(BF16).astype(F32)


def rows_iota():
    return lax.broadcasted_iota(jnp.int32, (8, 128), 0)


def sel4(a, b, c, d):
    k = rows_iota() & 3
    return jnp.where(k == 0, a, jnp.where(k == 1, b, jnp.where(k == 2, c, d)))


def spread(row):
    return jnp.broadcast_to(row, (8, 128))


def read3(ref, c, first=0):
    return [spread(ref[c, first + a : first + a + 1, :]) for a in range(3)]


def centred(xs, centre):
    return [x - centre[a] for a, x in enumerate(xs)]


def products(xs, last4):
    ri = rows_iota()
    one_x0 = jnp.where(ri < 4, 1.0, xs[0])
    x1_x2 = jnp.where(ri < 4, xs[1], xs[2])
    return one_x0 * last4, x1_x2 * last4


def dot3(a, b):
    return a[0] * b[0] + a[1] * b[1] + a[2] * b[2]


def put_features(ref, c, xs, vs, with_self):
    groups = list(products(xs, sel4(vs[0], vs[1], vs[2], dot3(xs, vs))))
    if with_self:
        groups += list(products(xs, sel4(xs[0], xs[1], xs[2], 1.0)))
    x = jnp.concatenate(groups, axis=0)
    h, m, low = split3(x)
    ref[c // 2, :, 128 * (c % 2) : 128 * (c % 2) + 128] = jnp.concatenate([h, m, low], axis=0).astype(BF16)


def put_far_side(ref, c, xs):
    ri = rows_iota()
    h, m, low = split3(sel4(xs[0], xs[1], xs[2], dot3(xs, xs)))
    mark = (lax.broadcasted_iota(jnp.int32, (FEATS, 128), 0) == c).astype(F32)
    x = jnp.concatenate([h, m, jnp.where(ri < 4, low, 1.0), h, mark], axis=0)
    ref[c] = x.T.astype(BF16)


def put_own_side(ref, b, xs, dead):
    ri = rows_iota()
    h, m, low = split3(sel4(xs[0], xs[1], xs[2], 0.0))
    nh, nm, nl = split3(1.0 + dot3(xs, xs))
    first = jnp.where(ri == 3, 1.0, jnp.where(ri < 4, -2.0 * h, -2.0 * m))
    first = jnp.where(ri == 7, 0.0, first)
    third = jnp.where(ri < 3, -2.0 * h, jnp.where(ri == 3, 1.0, sel4(nh, nm, nl, 0.0)))
    fourth = jnp.where(ri < 3, -2.0 * low, 0.0)
    x = jnp.concatenate([first, first, third, fourth, dead], axis=0)
    ref[b // 2, :, 128 * (b % 2) : 128 * (b % 2) + 128] = x.astype(BF16)


def dead_rows(near_ref, mask_ref, b, base, slots):
    h = lax.broadcasted_iota(jnp.int32, (FEATS, slots), 0)
    near = jnp.broadcast_to(near_ref[b : b + 1, :], (FEATS, slots))
    live = jnp.broadcast_to(mask_ref[b : b + 1, :], (FEATS, slots)) > 0
    hit = jnp.where(live & (near == base(h)), 1.0, 0.0)
    found = jnp.max(hit, axis=1, keepdims=True)
    return jnp.broadcast_to((1.0 - found) * DEAD, (FEATS, 128))


def pair_weights(far, own):
    s = jnp.dot(far, own, preferred_element_type=F32)
    r = 1.0 / s
    w = r * r
    hi = w.astype(BF16)
    return hi, (w - hi.astype(F32)).astype(BF16)


def fold(acc, n):
    both = acc[:, :128] + acc[:, 128:]
    return (both[:n] + both[n : 2 * n] + both[2 * n :]) * (1.0 / 128)


def first_product(weights_ref, far_side, own_side, feats, put, pairs, window):
    def step(p, carry):
        own = own_side[p]
        start = p if window else 0
        accs = [jnp.zeros((3 * FEATS, 256), F32) for _ in range(2)]
        for t in range(pairs):
            parts = [[], []]
            for cc in range(2):
                hi, lo = pair_weights(far_side[2 * (start + t) + cc], own)
                for q in range(2):
                    cut = slice(128 * q, 128 * q + 128)
                    parts[q].append(jnp.concatenate([hi[:, cut], lo[:, cut]], axis=1))
            f = feats[start + t]
            for q in range(2):
                tile = jnp.concatenate(parts[q], axis=0)
                weights_ref[2 * p + q, t] = tile
                accs[q] = accs[q] + jnp.dot(f, tile, preferred_element_type=F32)
        for q in range(2):
            put(2 * p + q, fold(accs[q], FEATS))
        return carry

    lax.fori_loop(0, pairs, step, 0)


def second_product(weights_ref, feats, put, pairs, window):
    def step(p, carry):
        start = p if window else 0
        for q in range(2):
            acc = jnp.zeros((3 * FEATS // 2, 256), F32)
            for t in range(pairs):
                acc = acc + jnp.dot(feats[start + t], weights_ref[2 * p + q, t], preferred_element_type=F32)
            put(2 * p + q, fold(acc, FEATS // 2))
        return carry

    lax.fori_loop(0, pairs, step, 0)


def apply_local(field, feld_self, xs, vs, stiff, residual_rows):
    q = dot3(xs, vs)
    vpat = sel4(vs[0], vs[1], vs[2], -q)
    xpat = sel4(xs[0], xs[1], xs[2], -1.0)
    g01 = feld_self[0:8] * vpat + field[0:8] * xpat
    g23 = feld_self[8:16] * vpat + field[8:16] * xpat
    z = [jnp.sum(g, axis=0, keepdims=True) for g in (g01[0:4], g01[4:8], g23[0:4], g23[4:8])]
    for a in range(3):
        residual_rows(a, stiff * vs[a][0:1] + z[a + 1] - xs[a][0:1] * z[0])


def local_first(coords, force, near, mask, weights, field, centre_out, far_side, own_side, feats):
    blocks, _, atoms = coords.shape
    slots = near.shape[1]
    first_block = lax.axis_index("space") * blocks
    total = coords[0]
    for b in range(1, blocks):
        total = total + coords[b]
    mean = jnp.sum(total, axis=1, keepdims=True) * (1.0 / (blocks * atoms))
    centre = [jnp.broadcast_to(mean[a : a + 1], (8, 128)) for a in range(3)]
    for a in range(3):
        centre_out[8 * a : 8 * a + 8] = centre[a]
    for b in range(blocks):
        xs = centred(read3(coords, b), centre)
        put_far_side(far_side, b, xs)
        put_features(feats, b, xs, read3(force, b), True)
        put_own_side(own_side, b, xs, dead_rows(near, mask, b, lambda h: h + first_block, slots))

    def put(b, value):
        field[b] = value

    first_product(weights, far_side, own_side, feats, put, blocks // 2, False)


def get_centre(ref):
    return [ref[8 * a : 8 * a + 8] for a in range(3)]


def halo(left, right, c, blocks):
    return (left, c + 1) if c < blocks - 1 else (right, c - (blocks - 1))


def halo_first(left, right, coords, force, stiff, near, mask, centre_in, field_in, weights, selfs, image, far_side, own_side, feats):
    blocks = coords.shape[0]
    slots = near.shape[1]
    first_block = lax.axis_index("space") * blocks
    centre = get_centre(centre_in)
    base = lambda h: first_block + h + jnp.where(h < blocks - 1, 1 - blocks, 1)
    for c in range(2 * (blocks - 1)):
        ref, k = halo(left, right, c, blocks)
        xs = centred(read3(ref, k), centre)
        put_far_side(far_side, c, xs)
        put_features(feats, c, xs, read3(ref, k, 3), True)
    for b in range(blocks):
        xs = centred(read3(coords, b), centre)
        put_own_side(own_side, b, xs, dead_rows(near, mask, b, base, slots))

    def put(b, value):
        value = value + field_in[b]
        half = FEATS // 2
        selfs[b] = value[half:]
        xs = centred(read3(coords, b), centre)

        def rows(a, row):
            image[b, a : a + 1, :] = row

        apply_local(value[:half], value[half:], xs, read3(force, b), stiff[pl.ds(b, 1), :], rows)

    first_product(weights, far_side, own_side, feats, put, blocks // 2, True)


def local_second(coords, vector, centre_in, weights, field, feats):
    blocks = coords.shape[0]
    centre = get_centre(centre_in)
    for b in range(blocks):
        put_features(feats, b, centred(read3(coords, b), centre), read3(vector, b), False)

    def put(b, value):
        field[b] = value

    second_product(weights, feats, put, blocks // 2, False)


def total(x):
    return jnp.sum(jnp.sum(x, axis=0, keepdims=True), axis=1, keepdims=True)


def halo_second(vleft, vright, left, right, coords, vector, force, stiff, centre_in, selfs, field_in, weights, image, sums, feats):
    blocks = coords.shape[0]
    centre = get_centre(centre_in)
    for c in range(2 * (blocks - 1)):
        ref, k = halo(left, right, c, blocks)
        vref, _ = halo(vleft, vright, c, blocks)
        put_features(feats, c, centred(read3(ref, k), centre), read3(vref, k), False)

    def put(b, value):
        value = value + field_in[b]
        xs = centred(read3(coords, b), centre)

        def rows(a, row):
            image[b, a : a + 1, :] = row

        apply_local(value, selfs[b], xs, read3(vector, b), stiff[pl.ds(b, 1), :], rows)

    second_product(weights, feats, put, blocks // 2, True)
    s00 = s01 = jnp.zeros(force.shape[1:], F32)
    for b in range(blocks):
        f, v = force[b], vector[b]
        s00 = s00 + f * f
        s01 = s01 + f * v
    s00, s01 = total(s00), total(s01)
    shift = s01 / jnp.maximum(s00, 1e-30)
    parts = [jnp.zeros(force.shape[1:], F32) for _ in range(4)]
    for b in range(blocks):
        f, v, w = force[b], vector[b], image[b]
        u = v - shift * f
        w = w - shift * v
        for k, term in enumerate((f * u, u * u, f * w + u * v, u * w)):
            parts[k] = parts[k] + term
    values = [s00, s01, shift] + [total(x) for x in parts]
    lane = lax.broadcasted_iota(jnp.int32, sums.shape, 1)
    row = jnp.zeros(sums.shape, F32)
    for k, value in enumerate(values):
        row = jnp.where(lane == k, value, row)
    sums[...] = row


def finish(sums, force, image, image2, solution_out, residual_out):
    table = sums[...]
    s00, s01, shift, s0u, suu, cross, suw = [table[:, k : k + 1] for k in range(7)]
    add = lambda x: jnp.sum(x, axis=0, keepdims=True)
    norm = add(s00)
    alpha = norm / add(s01)
    e = 1.0 - alpha * shift
    norm1 = add(e * e * s00 - 2.0 * alpha * e * s0u + alpha * alpha * suu)
    curve = add(e * e * s01 - alpha * e * cross + alpha * alpha * suw)
    beta = norm1 / norm
    step = norm1 / (curve - beta * norm1 / alpha)
    for b in range(force.shape[0]):
        f, v, w = force[b], image[b], image2[b]
        r = f - alpha * v
        solution_out[b] = alpha * f + step * (r + beta * f)
        residual_out[b] = r - step * (v - alpha * w + beta * v)


def params():
    return pltpu.CompilerParams(vmem_limit_bytes=8 * 2 ** 20)


def call(kernel, outs, args, scratch=()):
    return pl.pallas_call(
        kernel,
        out_shape=[jax.ShapeDtypeStruct(s, d) for s, d in outs],
        in_specs=[vmem()] * len(args),
        out_specs=[vmem()] * len(outs),
        scratch_shapes=[pltpu.VMEM(s, d) for s, d in scratch],
        compiler_params=params(),
    )(*args)


def per_device(coords, force, restraint, neighbors, mask):
    blocks, _, atoms = coords.shape
    devices = lax.axis_size("space")
    up = [(i, i + 1) for i in range(devices - 1)]
    down = [(i + 1, i) for i in range(devices - 1)]
    both = jnp.concatenate([coords, force], axis=1)
    left = lax.ppermute(both, "space", up)
    right = lax.ppermute(both, "space", down)
    wshape = ((blocks, blocks // 2, 2 * atoms, 2 * atoms), BF16)
    own_scratch = ((blocks // 2, 2 * FEATS, 2 * atoms), BF16)
    far = blocks * 2 - 2
    vec = (coords.shape, F32)

    w1, field, centre = call(
        local_first,
        [wshape, ((blocks, FEATS, atoms), F32), ((24, 128), F32)],
        (coords, force, neighbors, mask),
        [((blocks, atoms, 2 * FEATS), BF16), own_scratch, ((blocks // 2, 3 * FEATS, 2 * atoms), BF16)],
    )
    w2, selfs, image = call(
        halo_first,
        [wshape, ((blocks, FEATS // 2, atoms), F32), vec],
        (left, right, coords, force, restraint, neighbors, mask, centre, field),
        [((far, atoms, 2 * FEATS), BF16), own_scratch, ((far // 2, 3 * FEATS, 2 * atoms), BF16)],
    )
    vleft = lax.ppermute(image, "space", up)
    vright = lax.ppermute(image, "space", down)
    (field2,) = call(
        local_second,
        [((blocks, FEATS // 2, atoms), F32)],
        (coords, image, centre, w1),
        [((blocks // 2, 3 * FEATS // 2, 2 * atoms), BF16)],
    )
    image2, sums = call(
        halo_second,
        [vec, ((devices, 128), F32)],
        (vleft, vright, left, right, coords, image, force, restraint, centre, selfs, field2, w2),
        [((far // 2, 3 * FEATS // 2, 2 * atoms), BF16)],
    )
    table = lax.all_to_all(sums, "space", 0, 0, tiled=True)
    solved, residual = call(finish, [vec, vec], (table, force, image, image2))
    return solved, residual


def solution(mesh):
    in_specs = (
        P("space", None, None),
        P("space", None, None),
        P("space", None),
        P("space", None),
        P("space", None),
    )
    out_specs = (P("space", None, None), P("space", None, None))
    return jax.shard_map(per_device, mesh=mesh, in_specs=in_specs, out_specs=out_specs, check_vma=False)
```

time: 287 us -> 72.4 us (0.25)
  other arithmetic: 106 us -> 0.02 us
  blocking collectives: 88.4 us -> 16.7 us
  local copies, waits for them, and re-layouts: 65.1 us -> 6.2 us
  Pallas kernels: 0 us -> 37.4 us
  between operations: 6.58 us -> 0.75 us
  waiting for transfers between devices: 4.29 us -> 0.01 us
    psum x2 -> x0, blocking collectives: 88.4 us -> none  [two_sums(): lax.psum((jnp.sum(residual * residual), jnp.sum(residual * image)), 'space')]
    reduce_sum x67 -> x0, other arithmetic: 87.5 us -> none  [the longest x32 57.7 us: block_product(): squared = jnp.sum(offset * offset, axis=1)]
    gather x64 -> x0, local copies, waits for them, and re-layouts: 38.9 us -> none  [the longest x32 19.5 us: one_block(): coord_table[near_rows]]
    pallas_call x0 -> x5, Pallas kernels: none -> 37.4 us  [call(): pl.pallas_call(kernel, out_shape=[jax.ShapeDtypeStruct(s, d) for s, d in...]
    mul x32 -> x0, local copies, waits for them, and re-layouts: 22.3 us -> none  [block_product(): return own_spring[None, :] * own_values + pulled]
    all_to_all x0 -> x1, blocking collectives: none -> 16.7 us  [per_device(): table = lax.all_to_all(sums, 'space', 0, 0, tiled=True)]
    mul x32 -> x0, other arithmetic: 15.7 us -> none  [block_product(): strength = weight * motion]
    ppermute x6 -> x4, waiting for transfers between devices: 4.29 us -> 0.01 us  [the longest x1 0.01 us: per_device(): left = lax.ppermute(both, 'space', up)]
  transfers between devices with their start and end apart: 6 -> 4, of which waited for: 1 -> 0; matrix products, arithmetic and copies ran while one was open for 2% -> 0% of each run, Pallas kernels for 0% -> 25%
where the time goes in v1:
time: 72.4 us; the launch traced here: 71.9 us
  Pallas kernels  37.4 us (52%)
  blocking collectives  16.7 us (23%)
  starting transfers between devices  10.7 us (15%)
  local copies, waits for them, and re-layouts  6.2 us (9%)
  between operations  0.75 us (1%)
    pallas_call x5, Pallas kernels, call(): pl.pallas_call(kernel, out_shape=[jax.ShapeDtypeStruct(s, d) for s, d in...  37.4 us
    all_to_all x1, blocking collectives, per_device(): table = lax.all_to_all(sums, 'space', 0, 0, tiled=True)  16.7 us
    ppermute x1, starting transfers between devices, per_device(): vleft = lax.ppermute(image, 'space', up)  5.12 us
    unnamed x12, local copies, waits for them, and re-layouts  4.98 us
    ppermute x1, starting transfers between devices, per_device(): left = lax.ppermute(both, 'space', up)  3.03 us
  transfers between devices with their start and end apart: 4, of which 0 were waited for; matrix products, arithmetic and copies ran while one was open for 0% of the time, Pallas kernels for 25%

profile of v1, /device:TPU:0, one launch (start us, length us, event | category | flops | bytes accessed | tf_op | source)
XLA Modules:
  0.0 71.9 jit_solution(16341467035700360443)
XLA Ops:
  0.6 0.8 %copy.19.coords = f32[16,3,128]{2,1,0:T(4,128)S(1)} copy(f32[16,3,128]{2,0,1:T(8,128)} %param.5) | data formatting | bytes 49152 | tf_op args[0]
  1.4 0.8 %copy.20.force = f32[16,3,128]{2,1,0:T(4,128)S(1)} copy(f32[16,3,128]{2,0,1:T(8,128)} %param.6) | data formatting | bytes 49152 | tf_op args[1]
  2.2 1.3 %collective-permute-start.1 = (f32[16,6,128]{2,1,0:T(8,128)S(1)}, f32[16,6,128]{2,1,0:T(8,128)S(1)}, u32[]{:S(2)}, u32[]{:S(2)}) collective-permute-start(f32[16,6,128]{2,1,0:T(8,128)S(1)} %pad_maximum_fusion), channel_id=1, source_target_pairs={{1,0},{2,1},{3,2},{4,3},{5,4},{6,5},{7,6},{8,7},{9,8},{10,9},{11,1... | collective-permute-start | bytes 147464 | tf_op jit(solution)/shard_map/ppermute | solution.py:313
  3.5 3.0 %collective-permute-start = (f32[16,6,128]{2,1,0:T(8,128)S(1)}, f32[16,6,128]{2,1,0:T(8,128)S(1)}, u32[]{:S(2)}, u32[]{:S(2)}) collective-permute-start(f32[16,6,128]{2,1,0:T(8,128)S(1)} %pad_maximum_fusion), channel_id=1, source_target_pairs={{0,1},{1,2},{2,3},{3,4},{4,5},{5,6},{6,7},{7,8},{8,9},{9,10},{10,1... | collective-permute-start | bytes 147464 | tf_op jit(solution)/shard_map/ppermute | solution.py:312
  6.5 0.0 copy-start.1
  6.5 0.7 copy-done.1
  7.2 0.7 copy-done.3
  7.9 14.4 %shard_map.68 = (bf16[16,8,256,256]{3,2,1,0:T(8,128)(2,1)S(1)}, f32[16,32,128]{2,1,0:T(8,128)S(1)}, f32[24,128]{1,0:T(8,128)S(1)}) custom-call(f32[16,3,128]{2,1,0:T(4,128)S(1)} %copy.19.coords, f32[16,3,128]{2,1,0:T(4,128)S(1)} %copy.20.force, s32[16,32]{1,0:T(8,128)S(1)} %copy-done.1, s32[16,32]{1,0:T(8,128)S(1)} %copy-done.3), custom_call_target="tpu_custom_call" | custom-call | tf_op jit(solution)/shard_map/pallas_call | solution.py:296
  22.3 0.0 collective-permute-done.1.right
  22.3 0.0 collective-permute-done.left
  22.3 0.0 copy-start
  22.3 0.7 copy-done
  23.0 0.7 copy-done.2
  23.7 0.7 copy-done.4
  24.4 14.6 %shard_map.69 = (bf16[16,8,256,256]{3,2,1,0:T(8,128)(2,1)S(1)}, f32[16,16,128]{2,1,0:T(8,128)S(1)}, f32[16,3,128]{2,1,0:T(4,128)S(1)}) custom-call(f32[16,6,128]{2,1,0:T(8,128)S(1)} %collective-permute-done.left, f32[16,6,128]{2,1,0:T(8,128)S(1)} %collective-permute-done.1.right, f32[16,3,128]{2,1,0:T(4,128)S(1)} %copy.19.coords, ...), custom_call_target="tpu_custom_call" | custom-call | tf_op jit(solution)/shard_map/pallas_call | solution.py:296
  39.0 1.3 %collective-permute-start.3 = (f32[16,3,128]{2,1,0:T(4,128)S(1)}, f32[16,3,128]{2,1,0:T(4,128)S(1)}, u32[]{:S(2)}, u32[]{:S(2)}) collective-permute-start(f32[16,3,128]{2,1,0:T(4,128)S(1)} %get-tuple-element.12.vector.image), channel_id=1, source_target_pairs={{1,0},{2,1},{3,2},{4,3},{5,4},{6,5},{7,6},{8,7},{9,8},{10,9},{11,1... | collective-permute-start | bytes 73736 | tf_op jit(solution)/shard_map/ppermute | solution.py:332
  40.3 5.1 %collective-permute-start.2 = (f32[16,3,128]{2,1,0:T(4,128)S(1)}, f32[16,3,128]{2,1,0:T(4,128)S(1)}, u32[]{:S(2)}, u32[]{:S(2)}) collective-permute-start(f32[16,3,128]{2,1,0:T(4,128)S(1)} %get-tuple-element.12.vector.image), channel_id=1, source_target_pairs={{0,1},{1,2},{2,3},{3,4},{4,5},{5,6},{6,7},{7,8},{8,9},{9,10},{10,1... | collective-permute-start | bytes 73736 | tf_op jit(solution)/shard_map/ppermute | solution.py:331
  45.4 3.9 %shard_map.70.field_in = f32[16,16,128]{2,1,0:T(8,128)S(1)} custom-call(f32[16,3,128]{2,1,0:T(4,128)S(1)} %copy.19.coords, f32[16,3,128]{2,1,0:T(4,128)S(1)} %get-tuple-element.12.vector.image, f32[24,128]{1,0:T(8,128)S(1)} %get-tuple-element.10.centre_in, bf16[16,8,256,256]{3,2,1,0:T(8,128)(2,1)S(1)} %get-tuple-element.14.weights), custom_call_target="tpu_custom_call" | custom-call | tf_op jit(solution)/shard_map/pallas_call | solution.py:296
  49.4 0.0 collective-permute-done.2.vleft
  49.4 4.3 %shard_map.71 = (f32[16,3,128]{2,1,0:T(4,128)S(1)}, f32[32,128]{1,0:T(8,128)S(1)}) custom-call(f32[16,3,128]{2,1,0:T(4,128)S(1)} %collective-permute-done.2.vleft, f32[16,3,128]{2,1,0:T(4,128)S(1)} %collective-permute-done.3.vright, f32[16,6,128]{2,1,0:T(8,128)S(1)} %collective-permute-done.left, f32[16,6,128]{2,1,0:T(8,128)S(1)} %collective-permute-done.1.right, ...), custom_call_target="tpu_custom_call" | custom-call | tf_op jit(solution)/shard_map/pallas_call | solution.py:296
  53.7 16.7 %all_to_all.11 = f32[32,1,128]{2,1,0:T(1,128)S(1)} all-to-all(f32[32,1,128]{2,1,0:T(1,128)S(1)} %bitcast.5), channel_id=1, replica_groups=mesh['space'=32] {'space'}, dimensions={0} | all-to-all | bytes 32768 | tf_op jit(solution)/shard_map/all_to_all | solution.py:345
  70.4 0.2 shard_map.72
  70.6 0.6 copy.30
  71.3 0.6 copy.31
  (5 shorter events, 0.0 us)
Async XLA Ops:
  2.2 20.1 %collective-permute-start.1 = (f32[16,6,128]{2,1,0:T(8,128)S(1)}, f32[16,6,128]{2,1,0:T(8,128)S(1)}, u32[]{:S(2)}, u32[]{:S(2)}) collective-permute-start(f32[16,6,128]{2,1,0:T(8,128)S(1)} %pad_maximum_fusion), channel_id=1, source_target_pairs={{1,0},{2,1},{3,2},{4,3},{5,4},{6,5},{7,6},{8,7},{9,8},{10,9},{11,1... | collective-permute-start | bytes 147464 | tf_op jit(solution)/shard_map/ppermute | solution.py:313
  3.5 18.8 %collective-permute-start = (f32[16,6,128]{2,1,0:T(8,128)S(1)}, f32[16,6,128]{2,1,0:T(8,128)S(1)}, u32[]{:S(2)}, u32[]{:S(2)}) collective-permute-start(f32[16,6,128]{2,1,0:T(8,128)S(1)} %pad_maximum_fusion), channel_id=1, source_target_pairs={{0,1},{1,2},{2,3},{3,4},{4,5},{5,6},{6,7},{7,8},{8,9},{9,10},{10,1... | collective-permute-start | bytes 147464 | tf_op jit(solution)/shard_map/ppermute | solution.py:312
  6.5 0.7 copy-start.1
  7.2 0.7 copy-start.3
  22.3 0.7 copy-start
  23.0 0.7 copy-start.2
  23.7 0.7 copy-start.4
  39.0 10.4 %collective-permute-start.3 = (f32[16,3,128]{2,1,0:T(4,128)S(1)}, f32[16,3,128]{2,1,0:T(4,128)S(1)}, u32[]{:S(2)}, u32[]{:S(2)}) collective-permute-start(f32[16,3,128]{2,1,0:T(4,128)S(1)} %get-tuple-element.12.vector.image), channel_id=1, source_target_pairs={{1,0},{2,1},{3,2},{4,3},{5,4},{6,5},{7,6},{8,7},{9,8},{10,9},{11,1... | collective-permute-start | bytes 73736 | tf_op jit(solution)/shard_map/ppermute | solution.py:332
  40.3 9.1 %collective-permute-start.2 = (f32[16,3,128]{2,1,0:T(4,128)S(1)}, f32[16,3,128]{2,1,0:T(4,128)S(1)}, u32[]{:S(2)}, u32[]{:S(2)}) collective-permute-start(f32[16,3,128]{2,1,0:T(4,128)S(1)} %get-tuple-element.12.vector.image), channel_id=1, source_target_pairs={{0,1},{1,2},{2,3},{3,4},{4,5},{5,6},{6,7},{7,8},{8,9},{9,10},{10,1... | collective-permute-start | bytes 73736 | tf_op jit(solution)/shard_map/ppermute | solution.py:331

commit v2 on v1

--- a/solution.py
+++ b/solution.py
@@ -61,15 +61,16 @@
         groups += list(products(xs, sel4(xs[0], xs[1], xs[2], 1.0)))
     x = jnp.concatenate(groups, axis=0)
     h, m, low = split3(x)
-    ref[c // 2, :, 128 * (c % 2) : 128 * (c % 2) + 128] = jnp.concatenate([h, m, low], axis=0).astype(BF16)
+    ref[c] = jnp.concatenate([h, m, low], axis=0).astype(BF16)
 
 
 def put_far_side(ref, c, xs):
     ri = rows_iota()
     h, m, low = split3(sel4(xs[0], xs[1], xs[2], dot3(xs, xs)))
     mark = (lax.broadcasted_iota(jnp.int32, (FEATS, 128), 0) == c).astype(F32)
-    x = jnp.concatenate([h, m, jnp.where(ri < 4, low, 1.0), h, mark], axis=0)
-    ref[c] = x.T.astype(BF16)
+    rest = jnp.zeros((128 - 2 * FEATS, 128), F32)
+    x = jnp.concatenate([h, m, jnp.where(ri < 4, low, 1.0), h, mark, rest], axis=0)
+    ref[c] = x.astype(BF16).T
 
 
 def put_own_side(ref, b, xs, dead):
@@ -81,7 +82,7 @@
     third = jnp.where(ri < 3, -2.0 * h, jnp.where(ri == 3, 1.0, sel4(nh, nm, nl, 0.0)))
     fourth = jnp.where(ri < 3, -2.0 * low, 0.0)
     x = jnp.concatenate([first, first, third, fourth, dead], axis=0)
-    ref[b // 2, :, 128 * (b % 2) : 128 * (b % 2) + 128] = x.astype(BF16)
+    ref[b] = x.astype(BF16)
 
 
 def dead_rows(near_ref, mask_ref, b, base, slots):
@@ -93,54 +94,76 @@
     return jnp.broadcast_to((1.0 - found) * DEAD, (FEATS, 128))
 
 
-def pair_weights(far, own):
-    s = jnp.dot(far, own, preferred_element_type=F32)
-    r = 1.0 / s
-    w = r * r
-    hi = w.astype(BF16)
-    return hi, (w - hi.astype(F32)).astype(BF16)
-
-
 def fold(acc, n):
     both = acc[:, :128] + acc[:, 128:]
     return (both[:n] + both[n : 2 * n] + both[2 * n :]) * (1.0 / 128)
 
 
+def beside(a, b):
+    return jnp.concatenate([a, b], axis=1)
+
+
 def first_product(weights_ref, far_side, own_side, feats, put, pairs, window):
-    def step(p, carry):
-        own = own_side[p]
-        start = p if window else 0
-        accs = [jnp.zeros((3 * FEATS, 256), F32) for _ in range(2)]
-        for t in range(pairs):
-            parts = [[], []]
-            for cc in range(2):
-                hi, lo = pair_weights(far_side[2 * (start + t) + cc], own)
+    depth = 4
+
+    def body(*accs):
+        soft, outs = accs[:depth], accs[depth:]
+
+        def push_own(p):
+            own = beside(own_side[2 * p], own_side[2 * p + 1])
+            own = jnp.concatenate([own, jnp.zeros((256 - own.shape[0], 256), BF16)], axis=0)
+            pltpu.matmul_push_rhs(own, staging_register=p % 2, mxu_index=0)
+
+        push_own(0)
+        for p in range(pairs):
+            start = p if window else 0
+            for t in range(pairs):
+                parts = [[], []]
+                for cc in range(2):
+                    first = t + cc == 0
+                    far = far_side[2 * (start + t) + cc]
+                    acc = soft[(2 * t + cc) % depth]
+                    pltpu.matmul_acc_lhs(acc, beside(far, far), load_staged_rhs=p % 2 if first else None)
+                    if first and p + 1 < pairs:
+                        push_own(p + 1)
+                    r = 1.0 / pltpu.matmul_pop(acc)
+                    w = r * r
+                    hi = w.astype(BF16)
+                    lo = (w - hi.astype(F32)).astype(BF16)
+                    rows = slice(128 * cc, 128 * cc + 128)
+                    for q in range(2):
+                        cut = slice(128 * q, 128 * q + 128)
+                        weights_ref[2 * p + q, t, 0, rows] = hi[:, cut]
+                        weights_ref[2 * p + q, t, 1, rows] = lo[:, cut]
+                        parts[q].append(beside(hi[:, cut], lo[:, cut]))
+                f = beside(feats[2 * (start + t)], feats[2 * (start + t) + 1])
                 for q in range(2):
-                    cut = slice(128 * q, 128 * q + 128)
-                    parts[q].append(jnp.concatenate([hi[:, cut], lo[:, cut]], axis=1))
-            f = feats[start + t]
+                    pltpu.matmul_push_rhs(jnp.concatenate(parts[q], axis=0), staging_register=q, mxu_index=1)
+                    pltpu.matmul_acc_lhs(outs[2 * (p % 2) + q], f, load_staged_rhs=q)
             for q in range(2):
-                tile = jnp.concatenate(parts[q], axis=0)
-                weights_ref[2 * p + q, t] = tile
-                accs[q] = accs[q] + jnp.dot(f, tile, preferred_element_type=F32)
-        for q in range(2):
-            put(2 * p + q, fold(accs[q], FEATS))
-        return carry
-
-    lax.fori_loop(0, pairs, step, 0)
+                put(2 * p + q, fold(pltpu.matmul_pop(outs[2 * (p % 2) + q]), FEATS))
+
+    soft = [pltpu.ACC(0)((128, 256), F32) for _ in range(depth)]
+    outs = [pltpu.ACC(1)((3 * FEATS, 256), F32) for _ in range(4)]
+    pl.run_scoped(body, *soft, *outs)
 
 
 def second_product(weights_ref, feats, put, pairs, window):
-    def step(p, carry):
-        start = p if window else 0
-        for q in range(2):
-            acc = jnp.zeros((3 * FEATS // 2, 256), F32)
+    rows = 3 * FEATS // 2
+
+    def body(*accs):
+        for p in range(pairs):
+            start = p if window else 0
             for t in range(pairs):
-                acc = acc + jnp.dot(feats[start + t], weights_ref[2 * p + q, t], preferred_element_type=F32)
-            put(2 * p + q, fold(acc, FEATS // 2))
-        return carry
-
-    lax.fori_loop(0, pairs, step, 0)
+                f = beside(feats[2 * (start + t)], feats[2 * (start + t) + 1])
+                for q in range(2):
+                    tile = beside(weights_ref[2 * p + q, t, 0], weights_ref[2 * p + q, t, 1])
+                    pltpu.matmul_push_rhs(tile, staging_register=t % 2, mxu_index=q)
+                    pltpu.matmul_acc_lhs(accs[2 * q + p % 2], f, load_staged_rhs=t % 2)
+            for q in range(2):
+                put(2 * p + q, fold(pltpu.matmul_pop(accs[2 * q + p % 2]), FEATS // 2))
+
+    pl.run_scoped(body, *[pltpu.ACC(q)((rows, 256), F32) for q in (0, 0, 1, 1)])
 
 
 def apply_local(field, feld_self, xs, vs, stiff, residual_rows):
@@ -311,8 +334,8 @@
     both = jnp.concatenate([coords, force], axis=1)
     left = lax.ppermute(both, "space", up)
     right = lax.ppermute(both, "space", down)
-    wshape = ((blocks, blocks // 2, 2 * atoms, 2 * atoms), BF16)
-    own_scratch = ((blocks // 2, 2 * FEATS, 2 * atoms), BF16)
+    wshape = ((blocks, blocks // 2, 2, 2 * atoms, atoms), BF16)
+    own_scratch = ((blocks, 2 * FEATS, atoms), BF16)
     far = blocks * 2 - 2
     vec = (coords.shape, F32)
 
@@ -320,13 +343,13 @@
         local_first,
         [wshape, ((blocks, FEATS, atoms), F32), ((24, 128), F32)],
         (coords, force, neighbors, mask),
-        [((blocks, atoms, 2 * FEATS), BF16), own_scratch, ((blocks // 2, 3 * FEATS, 2 * atoms), BF16)],
+        [((blocks, atoms, atoms), BF16), own_scratch, ((blocks, 3 * FEATS, atoms), BF16)],
     )
     w2, selfs, image = call(
         halo_first,
         [wshape, ((blocks, FEATS // 2, atoms), F32), vec],
         (left, right, coords, force, restraint, neighbors, mask, centre, field),
-        [((far, atoms, 2 * FEATS), BF16), own_scratch, ((far // 2, 3 * FEATS, 2 * atoms), BF16)],
+        [((far, atoms, atoms), BF16), own_scratch, ((far, 3 * FEATS, atoms), BF16)],
     )
     vleft = lax.ppermute(image, "space", up)
     vright = lax.ppermute(image, "space", down)
@@ -334,13 +357,13 @@
         local_second,
         [((blocks, FEATS // 2, atoms), F32)],
         (coords, image, centre, w1),
-        [((blocks // 2, 3 * FEATS // 2, 2 * atoms), BF16)],
+        [((blocks, 3 * FEATS // 2, atoms), BF16)],
     )
     image2, sums = call(
         halo_second,
         [vec, ((devices, 128), F32)],
         (vleft, vright, left, right, coords, image, force, restraint, centre, selfs, field2, w2),
-        [((far // 2, 3 * FEATS // 2, 2 * atoms), BF16)],
+        [((far, 3 * FEATS // 2, atoms), BF16)],
     )
     table = lax.all_to_all(sums, "space", 0, 0, tiled=True)
     solved, residual = call(finish, [vec, vec], (table, force, image, image2))

time: 72.4 us -> 51.5 us (0.71)
  Pallas kernels: 37.4 us -> 16.3 us
    pallas_call x5, Pallas kernels: 37.4 us -> 16.3 us  [call(): pl.pallas_call(kernel, out_shape=[jax.ShapeDtypeStruct(s, d) for s, d in...]
  transfers between devices with their start and end apart: 4 -> 4, of which waited for: 0 -> 0; matrix products, arithmetic and copies ran while one was open for 0% -> 0% of each run, Pallas kernels for 25% -> 16%
where the time goes in v2:
time: 51.5 us; the launch traced here: 51 us
  blocking collectives  16.7 us (32%)
  Pallas kernels  16.3 us (32%)
  starting transfers between devices  10.9 us (21%)
  local copies, waits for them, and re-layouts  6.2 us (12%)
  between operations  0.75 us (1%)
    all_to_all x1, blocking collectives, per_device(): table = lax.all_to_all(sums, 'space', 0, 0, tiled=True)  16.7 us
    pallas_call x5, Pallas kernels, call(): pl.pallas_call(kernel, out_shape=[jax.ShapeDtypeStruct(s, d) for s, d in...  16.3 us
    ppermute x1, starting transfers between devices, per_device(): vleft = lax.ppermute(image, 'space', up)  5.31 us
    unnamed x12, local copies, waits for them, and re-layouts  4.98 us
    ppermute x1, starting transfers between devices, per_device(): left = lax.ppermute(both, 'space', up)  3.03 us
    ppermute x1, starting transfers between devices, per_device(): right = lax.ppermute(both, 'space', down)  1.29 us
    ppermute x1, starting transfers between devices, per_device(): vright = lax.ppermute(image, 'space', down)  1.29 us
    pallas_call x2, local copies, waits for them, and re-layouts, call(): pl.pallas_call(kernel, out_shape=[jax.ShapeDtypeStruct(s, d) for s, d in...  1.22 us
  transfers between devices with their start and end apart: 4, of which 0 were waited for; matrix products, arithmetic and copies ran while one was open for 0% of the time, Pallas kernels for 16%

profile of v2, /device:TPU:0, one launch (start us, length us, event | category | flops | bytes accessed | tf_op | source)
XLA Modules:
  0.0 51.0 jit_solution(11355597641679190772)
XLA Ops:
  0.6 0.8 %copy.19.coords = f32[16,3,128]{2,1,0:T(4,128)S(1)} copy(f32[16,3,128]{2,0,1:T(8,128)} %param.5) | data formatting | bytes 49152 | tf_op args[0]
  1.4 0.8 %copy.20.force = f32[16,3,128]{2,1,0:T(4,128)S(1)} copy(f32[16,3,128]{2,0,1:T(8,128)} %param.6) | data formatting | bytes 49152 | tf_op args[1]
  2.2 1.3 %collective-permute-start.1 = (f32[16,6,128]{2,1,0:T(8,128)S(1)}, f32[16,6,128]{2,1,0:T(8,128)S(1)}, u32[]{:S(2)}, u32[]{:S(2)}) collective-permute-start(f32[16,6,128]{2,1,0:T(8,128)S(1)} %pad_maximum_fusion), channel_id=1, source_target_pairs={{1,0},{2,1},{3,2},{4,3},{5,4},{6,5},{7,6},{8,7},{9,8},{10,9},{11,1... | collective-permute-start | bytes 147464 | tf_op jit(solution)/shard_map/ppermute | solution.py:336
  3.5 3.0 %collective-permute-start = (f32[16,6,128]{2,1,0:T(8,128)S(1)}, f32[16,6,128]{2,1,0:T(8,128)S(1)}, u32[]{:S(2)}, u32[]{:S(2)}) collective-permute-start(f32[16,6,128]{2,1,0:T(8,128)S(1)} %pad_maximum_fusion), channel_id=1, source_target_pairs={{0,1},{1,2},{2,3},{3,4},{4,5},{5,6},{6,7},{7,8},{8,9},{9,10},{10,1... | collective-permute-start | bytes 147464 | tf_op jit(solution)/shard_map/ppermute | solution.py:335
  6.5 0.0 copy-start.1
  6.5 0.7 %copy-done.1 = s32[16,32]{1,0:T(8,128)S(1)} copy-done((s32[16,32]{1,0:T(8,128)S(1)}, s32[16,32]{1,0:T(8,128)}, u32[]{:S(2)}) %copy-start.1) | copy-done | bytes 2072
  7.2 0.7 %copy-done.3 = s32[16,32]{1,0:T(8,128)S(1)} copy-done((s32[16,32]{1,0:T(8,128)S(1)}, s32[16,32]{1,0:T(8,128)}, u32[]{:S(2)}) %copy-start.3) | copy-done | bytes 2072
  7.9 5.0 %shard_map.68 = (bf16[16,8,2,256,128]{4,3,2,1,0:T(8,128)(2,1)S(1)}, f32[16,32,128]{2,1,0:T(8,128)S(1)}, f32[24,128]{1,0:T(8,128)S(1)}) custom-call(f32[16,3,128]{2,1,0:T(4,128)S(1)} %copy.19.coords, f32[16,3,128]{2,1,0:T(4,128)S(1)} %copy.20.force, s32[16,32]{1,0:T(8,128)S(1)} %copy-done.1, s32[16,32]{1,0:T(8,128)S(1)} %copy-done.3), custom_call_target="tpu_custom_call" | custom-call | tf_op jit(solution)/shard_map/pallas_call | solution.py:319
  12.9 0.0 collective-permute-done.1.right
  13.0 0.0 collective-permute-done.left
  13.0 0.0 copy-start
  13.0 0.7 %copy-done = f32[16,128]{1,0:T(8,128)S(1)} copy-done((f32[16,128]{1,0:T(8,128)S(1)}, f32[16,128]{1,0:T(8,128)}, u32[]{:S(2)}) %copy-start) | copy-done | bytes 8216
  13.7 0.7 %copy-done.2 = s32[16,32]{1,0:T(8,128)S(1)} copy-done((s32[16,32]{1,0:T(8,128)S(1)}, s32[16,32]{1,0:T(8,128)}, u32[]{:S(2)}) %copy-start.2) | copy-done | bytes 2072
  14.4 0.7 %copy-done.4 = s32[16,32]{1,0:T(8,128)S(1)} copy-done((s32[16,32]{1,0:T(8,128)S(1)}, s32[16,32]{1,0:T(8,128)}, u32[]{:S(2)}) %copy-start.4) | copy-done | bytes 2072
  15.1 5.1 %shard_map.69 = (bf16[16,8,2,256,128]{4,3,2,1,0:T(8,128)(2,1)S(1)}, f32[16,16,128]{2,1,0:T(8,128)S(1)}, f32[16,3,128]{2,1,0:T(4,128)S(1)}) custom-call(f32[16,6,128]{2,1,0:T(8,128)S(1)} %collective-permute-done.left, f32[16,6,128]{2,1,0:T(8,128)S(1)} %collective-permute-done.1.right, f32[16,3,128]{2,1,0:T(4,128)S(1)} %copy.19.coords, ...), custom_call_target="tpu_custom_call" | custom-call | tf_op jit(solution)/shard_map/pallas_call | solution.py:319
  20.2 1.3 %collective-permute-start.3 = (f32[16,3,128]{2,1,0:T(4,128)S(1)}, f32[16,3,128]{2,1,0:T(4,128)S(1)}, u32[]{:S(2)}, u32[]{:S(2)}) collective-permute-start(f32[16,3,128]{2,1,0:T(4,128)S(1)} %get-tuple-element.12.vector.image), channel_id=1, source_target_pairs={{1,0},{2,1},{3,2},{4,3},{5,4},{6,5},{7,6},{8,7},{9,8},{10,9},{11,1... | collective-permute-start | bytes 73736 | tf_op jit(solution)/shard_map/ppermute | solution.py:355
  21.5 5.3 %collective-permute-start.2 = (f32[16,3,128]{2,1,0:T(4,128)S(1)}, f32[16,3,128]{2,1,0:T(4,128)S(1)}, u32[]{:S(2)}, u32[]{:S(2)}) collective-permute-start(f32[16,3,128]{2,1,0:T(4,128)S(1)} %get-tuple-element.12.vector.image), channel_id=1, source_target_pairs={{0,1},{1,2},{2,3},{3,4},{4,5},{5,6},{6,7},{7,8},{8,9},{9,10},{10,1... | collective-permute-start | bytes 73736 | tf_op jit(solution)/shard_map/ppermute | solution.py:354
  26.8 2.9 %shard_map.70.field_in = f32[16,16,128]{2,1,0:T(8,128)S(1)} custom-call(f32[16,3,128]{2,1,0:T(4,128)S(1)} %copy.19.coords, f32[16,3,128]{2,1,0:T(4,128)S(1)} %get-tuple-element.12.vector.image, f32[24,128]{1,0:T(8,128)S(1)} %get-tuple-element.10.centre_in, bf16[16,8,2,256,128]{4,3,2,1,0:T(8,128)(2,1)S(1)} %get-tuple-element.14.weights), custom_call_target="tpu_custom_call" | custom-call | tf_op jit(solution)/shard_map/pallas_call | solution.py:319
  29.7 0.0 collective-permute-done.3.vright
  29.7 3.1 %shard_map.71 = (f32[16,3,128]{2,1,0:T(4,128)S(1)}, f32[32,128]{1,0:T(8,128)S(1)}) custom-call(f32[16,3,128]{2,1,0:T(4,128)S(1)} %collective-permute-done.2.vleft, f32[16,3,128]{2,1,0:T(4,128)S(1)} %collective-permute-done.3.vright, f32[16,6,128]{2,1,0:T(8,128)S(1)} %collective-permute-done.left, f32[16,6,128]{2,1,0:T(8,128)S(1)} %collective-permute-done.1.right, ...), custom_call_target="tpu_custom_call" | custom-call | tf_op jit(solution)/shard_map/pallas_call | solution.py:319
  32.8 16.7 %all_to_all.11 = f32[32,1,128]{2,1,0:T(1,128)S(1)} all-to-all(f32[32,1,128]{2,1,0:T(1,128)S(1)} %bitcast.5), channel_id=1, replica_groups=mesh['space'=32] {'space'}, dimensions={0} | all-to-all | bytes 32768 | tf_op jit(solution)/shard_map/all_to_all | solution.py:368
  49.5 0.2 shard_map.72
  49.7 0.6 %copy.30 = f32[16,3,128]{2,0,1:T(8,128)} copy(f32[16,3,128]{2,1,0:T(4,128)S(1)} %get-tuple-element.20) | data formatting | bytes 49152 | tf_op jit(solution)/shard_map/pallas_call | solution.py:319
  50.3 0.6 %copy.31 = f32[16,3,128]{2,0,1:T(8,128)} copy(f32[16,3,128]{2,1,0:T(4,128)S(1)} %get-tuple-element.21) | data formatting | bytes 49152 | tf_op jit(solution)/shard_map/pallas_call | solution.py:319
  (5 shorter events, 0.0 us)
Async XLA Ops:
  2.2 10.8 %collective-permute-start.1 = (f32[16,6,128]{2,1,0:T(8,128)S(1)}, f32[16,6,128]{2,1,0:T(8,128)S(1)}, u32[]{:S(2)}, u32[]{:S(2)}) collective-permute-start(f32[16,6,128]{2,1,0:T(8,128)S(1)} %pad_maximum_fusion), channel_id=1, source_target_pairs={{1,0},{2,1},{3,2},{4,3},{5,4},{6,5},{7,6},{8,7},{9,8},{10,9},{11,1... | collective-permute-start | bytes 147464 | tf_op jit(solution)/shard_map/ppermute | solution.py:336
  3.5 9.5 %collective-permute-start = (f32[16,6,128]{2,1,0:T(8,128)S(1)}, f32[16,6,128]{2,1,0:T(8,128)S(1)}, u32[]{:S(2)}, u32[]{:S(2)}) collective-permute-start(f32[16,6,128]{2,1,0:T(8,128)S(1)} %pad_maximum_fusion), channel_id=1, source_target_pairs={{0,1},{1,2},{2,3},{3,4},{4,5},{5,6},{6,7},{7,8},{8,9},{9,10},{10,1... | collective-permute-start | bytes 147464 | tf_op jit(solution)/shard_map/ppermute | solution.py:335
  6.5 0.7 %copy-start.1 = (s32[16,32]{1,0:T(8,128)S(1)}, s32[16,32]{1,0:T(8,128)}, u32[]{:S(2)}) copy-start(s32[16,32]{1,0:T(8,128)} %near.3) | copy-start | bytes 6148
  7.2 0.7 %copy-start.3 = (s32[16,32]{1,0:T(8,128)S(1)}, s32[16,32]{1,0:T(8,128)}, u32[]{:S(2)}) copy-start(s32[16,32]{1,0:T(8,128)} %mask.3) | copy-start | bytes 6148
  13.0 0.7 %copy-start = (f32[16,128]{1,0:T(8,128)S(1)}, f32[16,128]{1,0:T(8,128)}, u32[]{:S(2)}) copy-start(f32[16,128]{1,0:T(8,128)} %stiff.3) | copy-start | bytes 24580
  13.7 0.7 %copy-start.2 = (s32[16,32]{1,0:T(8,128)S(1)}, s32[16,32]{1,0:T(8,128)}, u32[]{:S(2)}) copy-start(s32[16,32]{1,0:T(8,128)} %near.3) | copy-start | bytes 6148
  14.4 0.7 %copy-start.4 = (s32[16,32]{1,0:T(8,128)S(1)}, s32[16,32]{1,0:T(8,128)}, u32[]{:S(2)}) copy-start(s32[16,32]{1,0:T(8,128)} %mask.3) | copy-start | bytes 6148
  20.2 9.5 %collective-permute-start.3 = (f32[16,3,128]{2,1,0:T(4,128)S(1)}, f32[16,3,128]{2,1,0:T(4,128)S(1)}, u32[]{:S(2)}, u32[]{:S(2)}) collective-permute-start(f32[16,3,128]{2,1,0:T(4,128)S(1)} %get-tuple-element.12.vector.image), channel_id=1, source_target_pairs={{1,0},{2,1},{3,2},{4,3},{5,4},{6,5},{7,6},{8,7},{9,8},{10,9},{11,1... | collective-permute-start | bytes 73736 | tf_op jit(solution)/shard_map/ppermute | solution.py:355
  21.5 8.2 %collective-permute-start.2 = (f32[16,3,128]{2,1,0:T(4,128)S(1)}, f32[16,3,128]{2,1,0:T(4,128)S(1)}, u32[]{:S(2)}, u32[]{:S(2)}) collective-permute-start(f32[16,3,128]{2,1,0:T(4,128)S(1)} %get-tuple-element.12.vector.image), channel_id=1, source_target_pairs={{0,1},{1,2},{2,3},{3,4},{4,5},{5,6},{6,7},{7,8},{8,9},{9,10},{10,1... | collective-permute-start | bytes 73736 | tf_op jit(solution)/shard_map/ppermute | solution.py:354

commit v3 on v2

--- a/solution.py
+++ b/solution.py
@@ -37,7 +37,7 @@
 
 
 def read3(ref, c, first=0):
-    return [spread(ref[c, first + a : first + a + 1, :]) for a in range(3)]
+    return [spread(ref[first + a, pl.ds(c, 1), :]) for a in range(3)]
 
 
 def centred(xs, centre):
@@ -177,21 +177,32 @@
         residual_rows(a, stiff * vs[a][0:1] + z[a + 1] - xs[a][0:1] * z[0])
 
 
-def local_first(coords, force, near, mask, weights, field, centre_out, far_side, own_side, feats):
-    blocks, _, atoms = coords.shape
+def stage(coords, force, stiff, near, mask, both_out, stiff_out, near_out, mask_out, sems):
+    copies = (
+        (coords, both_out.at[0:3]),
+        (force, both_out.at[3:6]),
+        (stiff, stiff_out),
+        (near, near_out),
+        (mask, mask_out),
+    )
+    started = [pltpu.make_async_copy(src, dst, sems.at[k]) for k, (src, dst) in enumerate(copies)]
+    for copy in started:
+        copy.start()
+    for copy in started:
+        copy.wait()
+
+
+def local_first(both, near, mask, weights, field, centre_out, far_side, own_side, feats):
+    _, blocks, atoms = both.shape
     slots = near.shape[1]
     first_block = lax.axis_index("space") * blocks
-    total = coords[0]
-    for b in range(1, blocks):
-        total = total + coords[b]
-    mean = jnp.sum(total, axis=1, keepdims=True) * (1.0 / (blocks * atoms))
-    centre = [jnp.broadcast_to(mean[a : a + 1], (8, 128)) for a in range(3)]
+    centre = [jnp.broadcast_to(total(both[a]) * (1.0 / (blocks * atoms)), (8, 128)) for a in range(3)]
     for a in range(3):
         centre_out[8 * a : 8 * a + 8] = centre[a]
     for b in range(blocks):
-        xs = centred(read3(coords, b), centre)
+        xs = centred(read3(both, b), centre)
         put_far_side(far_side, b, xs)
-        put_features(feats, b, xs, read3(force, b), True)
+        put_features(feats, b, xs, read3(both, b, 3), True)
         put_own_side(own_side, b, xs, dead_rows(near, mask, b, lambda h: h + first_block, slots))
 
     def put(b, value):
@@ -204,44 +215,52 @@
     return [ref[8 * a : 8 * a + 8] for a in range(3)]
 
 
-def halo(left, right, c, blocks):
-    return (left, c + 1) if c < blocks - 1 else (right, c - (blocks - 1))
-
-
-def halo_first(left, right, coords, force, stiff, near, mask, centre_in, field_in, weights, selfs, image, far_side, own_side, feats):
-    blocks = coords.shape[0]
+def order_halo(mate, other, ref):
+    odd = lax.rem(lax.axis_index("space"), 2) == 1
+    a, b = mate[...], other[...]
+    ref[0] = jnp.where(odd, a, b)
+    ref[1] = jnp.where(odd, b, a)
+
+
+def halo(ref, c, blocks):
+    return (ref.at[0], c + 1) if c < blocks - 1 else (ref.at[1], c - (blocks - 1))
+
+
+def halo_first(mate, other, both, stiff, near, mask, centre_in, field_in, weights, selfs, image, sides, far_side, own_side, feats):
+    _, blocks, _ = both.shape
     slots = near.shape[1]
     first_block = lax.axis_index("space") * blocks
     centre = get_centre(centre_in)
     base = lambda h: first_block + h + jnp.where(h < blocks - 1, 1 - blocks, 1)
+    order_halo(mate, other, sides)
     for c in range(2 * (blocks - 1)):
-        ref, k = halo(left, right, c, blocks)
+        ref, k = halo(sides, c, blocks)
         xs = centred(read3(ref, k), centre)
         put_far_side(far_side, c, xs)
         put_features(feats, c, xs, read3(ref, k, 3), True)
     for b in range(blocks):
-        xs = centred(read3(coords, b), centre)
+        xs = centred(read3(both, b), centre)
         put_own_side(own_side, b, xs, dead_rows(near, mask, b, base, slots))
 
     def put(b, value):
         value = value + field_in[b]
         half = FEATS // 2
         selfs[b] = value[half:]
-        xs = centred(read3(coords, b), centre)
+        xs = centred(read3(both, b), centre)
 
         def rows(a, row):
-            image[b, a : a + 1, :] = row
-
-        apply_local(value[:half], value[half:], xs, read3(force, b), stiff[pl.ds(b, 1), :], rows)
+            image[a, b : b + 1, :] = row
+
+        apply_local(value[:half], value[half:], xs, read3(both, b, 3), stiff[b : b + 1, :], rows)
 
     first_product(weights, far_side, own_side, feats, put, blocks // 2, True)
 
 
-def local_second(coords, vector, centre_in, weights, field, feats):
-    blocks = coords.shape[0]
+def local_second(both, vector, centre_in, weights, field, feats):
+    _, blocks, _ = both.shape
     centre = get_centre(centre_in)
     for b in range(blocks):
-        put_features(feats, b, centred(read3(coords, b), centre), read3(vector, b), False)
+        put_features(feats, b, centred(read3(both, b), centre), read3(vector, b), False)
 
     def put(b, value):
         field[b] = value
@@ -253,39 +272,33 @@
     return jnp.sum(jnp.sum(x, axis=0, keepdims=True), axis=1, keepdims=True)
 
 
-def halo_second(vleft, vright, left, right, coords, vector, force, stiff, centre_in, selfs, field_in, weights, image, sums, feats):
-    blocks = coords.shape[0]
+def halo_second(vmate, vother, mate, other, both, vector, stiff, centre_in, selfs, field_in, weights, image, sums, sides, vsides, feats):
+    _, blocks, _ = both.shape
     centre = get_centre(centre_in)
+    order_halo(mate, other, sides)
+    order_halo(vmate, vother, vsides)
     for c in range(2 * (blocks - 1)):
-        ref, k = halo(left, right, c, blocks)
-        vref, _ = halo(vleft, vright, c, blocks)
+        ref, k = halo(sides, c, blocks)
+        vref, _ = halo(vsides, c, blocks)
         put_features(feats, c, centred(read3(ref, k), centre), read3(vref, k), False)
 
     def put(b, value):
         value = value + field_in[b]
-        xs = centred(read3(coords, b), centre)
+        xs = centred(read3(both, b), centre)
 
         def rows(a, row):
-            image[b, a : a + 1, :] = row
-
-        apply_local(value, selfs[b], xs, read3(vector, b), stiff[pl.ds(b, 1), :], rows)
+            image[a, b : b + 1, :] = row
+
+        apply_local(value, selfs[b], xs, read3(vector, b), stiff[b : b + 1, :], rows)
 
     second_product(weights, feats, put, blocks // 2, True)
-    s00 = s01 = jnp.zeros(force.shape[1:], F32)
-    for b in range(blocks):
-        f, v = force[b], vector[b]
-        s00 = s00 + f * f
-        s01 = s01 + f * v
-    s00, s01 = total(s00), total(s01)
+    f, v, w = both[3:6], vector[...], image[...]
+    add = lambda x: total(jnp.sum(x, axis=0))
+    s00, s01 = add(f * f), add(f * v)
     shift = s01 / jnp.maximum(s00, 1e-30)
-    parts = [jnp.zeros(force.shape[1:], F32) for _ in range(4)]
-    for b in range(blocks):
-        f, v, w = force[b], vector[b], image[b]
-        u = v - shift * f
-        w = w - shift * v
-        for k, term in enumerate((f * u, u * u, f * w + u * v, u * w)):
-            parts[k] = parts[k] + term
-    values = [s00, s01, shift] + [total(x) for x in parts]
+    u = v - shift * f
+    w = w - shift * v
+    values = [s00, s01, shift, add(f * u), add(u * u), add(f * w + u * v), add(u * w)]
     lane = lax.broadcasted_iota(jnp.int32, sums.shape, 1)
     row = jnp.zeros(sums.shape, F32)
     for k, value in enumerate(values):
@@ -293,7 +306,7 @@
     sums[...] = row
 
 
-def finish(sums, force, image, image2, solution_out, residual_out):
+def finish(sums, both, image, image2, solution_out, residual_out, solution_buf, residual_buf, sems):
     table = sums[...]
     s00, s01, shift, s0u, suu, cross, suw = [table[:, k : k + 1] for k in range(7)]
     add = lambda x: jnp.sum(x, axis=0, keepdims=True)
@@ -304,70 +317,82 @@
     curve = add(e * e * s01 - alpha * e * cross + alpha * alpha * suw)
     beta = norm1 / norm
     step = norm1 / (curve - beta * norm1 / alpha)
-    for b in range(force.shape[0]):
-        f, v, w = force[b], image[b], image2[b]
-        r = f - alpha * v
-        solution_out[b] = alpha * f + step * (r + beta * f)
-        residual_out[b] = r - step * (v - alpha * w + beta * v)
-
-
-def params():
-    return pltpu.CompilerParams(vmem_limit_bytes=8 * 2 ** 20)
-
-
-def call(kernel, outs, args, scratch=()):
+    f, v, w = both[3:6], image[...], image2[...]
+    r = f - alpha * v
+    solution_buf[...] = alpha * f + step * (r + beta * f)
+    residual_buf[...] = r - step * (v - alpha * w + beta * v)
+    copies = [
+        pltpu.make_async_copy(solution_buf, solution_out, sems.at[0]),
+        pltpu.make_async_copy(residual_buf, residual_out, sems.at[1]),
+    ]
+    for copy in copies:
+        copy.start()
+    for copy in copies:
+        copy.wait()
+
+
+def call(kernel, outs, args, scratch=(), hbm_in=False, hbm_out=False, sems=0):
+    hbm = pl.BlockSpec(memory_space=pltpu.HBM)
     return pl.pallas_call(
         kernel,
         out_shape=[jax.ShapeDtypeStruct(s, d) for s, d in outs],
-        in_specs=[vmem()] * len(args),
-        out_specs=[vmem()] * len(outs),
-        scratch_shapes=[pltpu.VMEM(s, d) for s, d in scratch],
-        compiler_params=params(),
+        in_specs=[hbm if hbm_in else vmem()] * len(args),
+        out_specs=[hbm if hbm_out else vmem()] * len(outs),
+        scratch_shapes=[pltpu.VMEM(s, d) for s, d in scratch] + ([pltpu.SemaphoreType.DMA((sems,))] if sems else []),
+        compiler_params=pltpu.CompilerParams(vmem_limit_bytes=8 * 2 ** 20),
     )(*args)
 
 
 def per_device(coords, force, restraint, neighbors, mask):
-    blocks, _, atoms = coords.shape
+    blocks, parts, atoms = coords.shape
     devices = lax.axis_size("space")
-    up = [(i, i + 1) for i in range(devices - 1)]
-    down = [(i + 1, i) for i in range(devices - 1)]
-    both = jnp.concatenate([coords, force], axis=1)
-    left = lax.ppermute(both, "space", up)
-    right = lax.ppermute(both, "space", down)
+    mates = [(i, i ^ 1) for i in range(devices)]
+    others = [pair for i in range(1, devices - 1, 2) for pair in ((i, i + 1), (i + 1, i))]
+    flip = lambda x: jnp.transpose(x, (1, 0, 2))
+    vec = ((parts, blocks, atoms), F32)
+    pair = ((2 * parts, blocks, atoms), F32)
     wshape = ((blocks, blocks // 2, 2, 2 * atoms, atoms), BF16)
     own_scratch = ((blocks, 2 * FEATS, atoms), BF16)
     far = blocks * 2 - 2
-    vec = (coords.shape, F32)
-
+
+    both, stiff, near, live = call(
+        stage,
+        [pair, (restraint.shape, F32), (neighbors.shape, neighbors.dtype), (mask.shape, mask.dtype)],
+        [pltpu.with_memory_space_constraint(x, pltpu.HBM) for x in (flip(coords), flip(force), restraint, neighbors, mask)],
+        hbm_in=True,
+        sems=5,
+    )
+    other = lax.ppermute(both, "space", others)
+    mate = lax.ppermute(both, "space", mates)
     w1, field, centre = call(
         local_first,
         [wshape, ((blocks, FEATS, atoms), F32), ((24, 128), F32)],
-        (coords, force, neighbors, mask),
+        (both, near, live),
         [((blocks, atoms, atoms), BF16), own_scratch, ((blocks, 3 * FEATS, atoms), BF16)],
     )
     w2, selfs, image = call(
         halo_first,
         [wshape, ((blocks, FEATS // 2, atoms), F32), vec],
-        (left, right, coords, force, restraint, neighbors, mask, centre, field),
-        [((far, atoms, atoms), BF16), own_scratch, ((far, 3 * FEATS, atoms), BF16)],
-    )
-    vleft = lax.ppermute(image, "space", up)
-    vright = lax.ppermute(image, "space", down)
+        (mate, other, both, stiff, near, live, centre, field),
+        [((2,) + pair[0], F32), ((far, atoms, atoms), BF16), own_scratch, ((far, 3 * FEATS, atoms), BF16)],
+    )
+    vother = lax.ppermute(image, "space", others)
+    vmate = lax.ppermute(image, "space", mates)
     (field2,) = call(
         local_second,
         [((blocks, FEATS // 2, atoms), F32)],
-        (coords, image, centre, w1),
+        (both, image, centre, w1),
         [((blocks, 3 * FEATS // 2, atoms), BF16)],
     )
     image2, sums = call(
         halo_second,
         [vec, ((devices, 128), F32)],
-        (vleft, vright, left, right, coords, image, force, restraint, centre, selfs, field2, w2),
-        [((far, 3 * FEATS // 2, atoms), BF16)],
+        (vmate, vother, mate, other, both, image, stiff, centre, selfs, field2, w2),
+        [((2,) + pair[0], F32), ((2,) + vec[0], F32), ((far, 3 * FEATS // 2, atoms), BF16)],
     )
     table = lax.all_to_all(sums, "space", 0, 0, tiled=True)
-    solved, residual = call(finish, [vec, vec], (table, force, image, image2))
-    return solved, residual
+    solved, residual = call(finish, [vec, vec], (table, both, image, image2), [vec, vec], hbm_out=True, sems=2)
+    return flip(solved), flip(residual)
 
 
 def solution(mesh):

time: 51.5 us -> 39.7 us (0.77)
  local copies, waits for them, and re-layouts: 6.2 us -> 0 us
  blocking collectives: 16.7 us -> 12 us
  starting transfers between devices: 10.9 us -> 8.8 us
  Pallas kernels: 16.3 us -> 17.7 us
    unnamed x12 -> x0, local copies, waits for them, and re-layouts: 4.98 us -> none
    all_to_all x1, blocking collectives: 16.7 us -> 12 us  [per_device(): table = lax.all_to_all(sums, 'space', 0, 0, tiled=True)]
    ppermute x4, starting transfers between devices: 10.9 us -> 8.8 us  [the longest x1 4.39 us: per_device(): mate = lax.ppermute(both, 'space', mates)]
    pallas_call x5 -> x6, Pallas kernels: 16.3 us -> 17.7 us  [call(): pl.pallas_call(kernel, out_shape=[jax.ShapeDtypeStruct(s, d) for s, d in...]
    pallas_call x2 -> x0, local copies, waits for them, and re-layouts: 1.22 us -> none  [call(): pl.pallas_call(kernel, out_shape=[jax.ShapeDtypeStruct(s, d) for s, d in...]
  transfers between devices with their start and end apart: 4 -> 4, of which waited for: 0 -> 0; matrix products, arithmetic and copies ran while one was open for 0% -> 0% of each run, Pallas kernels for 16% -> 20%
where the time goes in v3:
time: 39.7 us; the launch traced here: 39.4 us
  Pallas kernels  17.7 us (45%)
  blocking collectives  12 us (30%)
  starting transfers between devices  8.8 us (22%)
  between operations  0.87 us (2%)
    pallas_call x6, Pallas kernels, call(): pl.pallas_call(kernel, out_shape=[jax.ShapeDtypeStruct(s, d) for s, d in...  17.7 us
    all_to_all x1, blocking collectives, per_device(): table = lax.all_to_all(sums, 'space', 0, 0, tiled=True)  12 us
    ppermute x1, starting transfers between devices, per_device(): mate = lax.ppermute(both, 'space', mates)  4.39 us
    ppermute x1, starting transfers between devices, per_device(): vmate = lax.ppermute(image, 'space', mates)  2.9 us
    ppermute x1, starting transfers between devices, per_device(): vother = lax.ppermute(image, 'space', others)  0.84 us
  transfers between devices with their start and end apart: 4, of which 0 were waited for; matrix products, arithmetic and copies ran while one was open for 0% of the time, Pallas kernels for 20%

profile of v3, /device:TPU:0, one launch (start us, length us, event | category | flops | bytes accessed | tf_op | source)
XLA Modules:
  0.0 39.4 jit_solution(5515260030437327581)
XLA Ops:
  0.6 0.8 %shard_map.68 = (f32[6,16,128]{2,1,0:T(8,128)S(1)}, f32[16,128]{1,0:T(8,128)S(1)}, s32[16,32]{1,0:T(8,128)S(1)}, s32[16,32]{1,0:T(8,128)S(1)}) custom-call(f32[3,16,128]{2,1,0:T(8,128)} %bitcast.10, f32[3,16,128]{2,1,0:T(8,128)} %bitcast.11, f32[16,128]{1,0:T(8,128)} %stiff.1, s32[16,32]{1,0:T(8,128)} %near.1, s32[16,32]{1,0:T(8,128)} %mask.1), custom_call_target="tpu_custom_call" | custom-call | tf_op jit(solution)/shard_map/pallas_call | solution.py:336
  1.4 0.7 %collective-permute-start.1 = (f32[6,16,128]{2,1,0:T(8,128)S(1)}, f32[6,16,128]{2,1,0:T(8,128)S(1)}, u32[]{:S(2)}, u32[]{:S(2)}) collective-permute-start(f32[6,16,128]{2,1,0:T(8,128)S(1)} %get-tuple-element.16.both), channel_id=1, source_target_pairs={{1,2},{2,1},{3,4},{4,3},{5,6},{6,5},{7,8},{8,7},{9,10},{10,9},{11,... | collective-permute-start | bytes 147464 | tf_op jit(solution)/shard_map/ppermute | solution.py:365
  2.1 4.4 %collective-permute-start = (f32[6,16,128]{2,1,0:T(8,128)S(1)}, f32[6,16,128]{2,1,0:T(8,128)S(1)}, u32[]{:S(2)}, u32[]{:S(2)}) collective-permute-start(f32[6,16,128]{2,1,0:T(8,128)S(1)} %get-tuple-element.16.both), channel_id=1, source_target_pairs={{0,1},{1,0},{2,3},{3,2},{4,5},{5,4},{6,7},{7,6},{8,9},{9,8},{10,11... | collective-permute-start | bytes 147464 | tf_op jit(solution)/shard_map/ppermute | solution.py:366
  6.5 5.0 %shard_map.69 = (bf16[16,8,2,256,128]{4,3,2,1,0:T(8,128)(2,1)S(1)}, f32[16,32,128]{2,1,0:T(8,128)S(1)}, f32[24,128]{1,0:T(8,128)S(1)}) custom-call(f32[6,16,128]{2,1,0:T(8,128)S(1)} %get-tuple-element.16.both, s32[16,32]{1,0:T(8,128)S(1)} %get-tuple-element.18.near, s32[16,32]{1,0:T(8,128)S(1)} %get-tuple-element.19.mask), custom_call_target="tpu_custom_call" | custom-call | tf_op jit(solution)/shard_map/pallas_call | solution.py:336
  11.5 0.0 collective-permute-done.1.other
  11.5 0.0 collective-permute-done.mate
  11.5 5.2 %shard_map.70 = (bf16[16,8,2,256,128]{4,3,2,1,0:T(8,128)(2,1)S(1)}, f32[16,16,128]{2,1,0:T(8,128)S(1)}, f32[3,16,128]{2,1,0:T(8,128)S(1)}) custom-call(f32[6,16,128]{2,1,0:T(8,128)S(1)} %collective-permute-done.mate, f32[6,16,128]{2,1,0:T(8,128)S(1)} %collective-permute-done.1.other, f32[6,16,128]{2,1,0:T(8,128)S(1)} %get-tuple-element.16.both, ...), custom_call_target="tpu_custom_call" | custom-call | tf_op jit(solution)/shard_map/pallas_call | solution.py:336
  16.7 0.8 %collective-permute-start.3 = (f32[3,16,128]{2,1,0:T(8,128)S(1)}, f32[3,16,128]{2,1,0:T(8,128)S(1)}, u32[]{:S(2)}, u32[]{:S(2)}) collective-permute-start(f32[3,16,128]{2,1,0:T(8,128)S(1)} %get-tuple-element.22.vector.image), channel_id=1, source_target_pairs={{1,2},{2,1},{3,4},{4,3},{5,6},{6,5},{7,8},{8,7},{9,10},{10,9},{11,... | collective-permute-start | bytes 73736 | tf_op jit(solution)/shard_map/ppermute | solution.py:379
  17.6 2.9 %collective-permute-start.2 = (f32[3,16,128]{2,1,0:T(8,128)S(1)}, f32[3,16,128]{2,1,0:T(8,128)S(1)}, u32[]{:S(2)}, u32[]{:S(2)}) collective-permute-start(f32[3,16,128]{2,1,0:T(8,128)S(1)} %get-tuple-element.22.vector.image), channel_id=1, source_target_pairs={{0,1},{1,0},{2,3},{3,2},{4,5},{5,4},{6,7},{7,6},{8,9},{9,8},{10,11... | collective-permute-start | bytes 73736 | tf_op jit(solution)/shard_map/ppermute | solution.py:380
  20.5 2.8 %shard_map.71.field_in = f32[16,16,128]{2,1,0:T(8,128)S(1)} custom-call(f32[6,16,128]{2,1,0:T(8,128)S(1)} %get-tuple-element.16.both, f32[3,16,128]{2,1,0:T(8,128)S(1)} %get-tuple-element.22.vector.image, f32[24,128]{1,0:T(8,128)S(1)} %get-tuple-element.20.centre_in, bf16[16,8,2,256,128]{4,3,2,1,0:T(8,128)(2,1)S(1)} %get-tuple-element.24.weights), custom_call_target="tpu_custom_call" | custom-call | tf_op jit(solution)/shard_map/pallas_call | solution.py:336
  23.3 0.0 collective-permute-done.3.vother
  23.3 0.0 collective-permute-done.2.vmate
  23.3 3.1 %shard_map.72 = (f32[3,16,128]{2,1,0:T(8,128)S(1)}, f32[32,128]{1,0:T(8,128)S(1)}) custom-call(f32[3,16,128]{2,1,0:T(8,128)S(1)} %collective-permute-done.2.vmate, f32[3,16,128]{2,1,0:T(8,128)S(1)} %collective-permute-done.3.vother, f32[6,16,128]{2,1,0:T(8,128)S(1)} %collective-permute-done.mate, f32[6,16,128]{2,1,0:T(8,128)S(1)} %collective-permute-done.1.other, ...), custom_call_target="tpu_custom_call" | custom-call | tf_op jit(solution)/shard_map/pallas_call | solution.py:336
  26.4 12.0 %all_to_all.11 = f32[32,1,128]{2,1,0:T(1,128)S(1)} all-to-all(f32[32,1,128]{2,1,0:T(1,128)S(1)} %bitcast.9), channel_id=1, replica_groups=mesh['space'=32] {'space'}, dimensions={0} | all-to-all | bytes 32768 | tf_op jit(solution)/shard_map/all_to_all | solution.py:393
  38.4 0.8 %shard_map.73 = (f32[3,16,128]{2,1,0:T(8,128)}, f32[3,16,128]{2,1,0:T(8,128)}) custom-call(f32[32,128]{1,0:T(8,128)S(1)} %bitcast.8, f32[6,16,128]{2,1,0:T(8,128)S(1)} %get-tuple-element.16.both, f32[3,16,128]{2,1,0:T(8,128)S(1)} %get-tuple-element.22.vector.image, f32[3,16,128]{2,1,0:T(8,128)S(1)} %get-tuple-element.27.image2), custom_call_target="tpu_custom_call" | custom-call | tf_op jit(solution)/shard_map/pallas_call | solution.py:336
Async XLA Ops:
  1.4 10.1 %collective-permute-start.1 = (f32[6,16,128]{2,1,0:T(8,128)S(1)}, f32[6,16,128]{2,1,0:T(8,128)S(1)}, u32[]{:S(2)}, u32[]{:S(2)}) collective-permute-start(f32[6,16,128]{2,1,0:T(8,128)S(1)} %get-tuple-element.16.both), channel_id=1, source_target_pairs={{1,2},{2,1},{3,4},{4,3},{5,6},{6,5},{7,8},{8,7},{9,10},{10,9},{11,... | collective-permute-start | bytes 147464 | tf_op jit(solution)/shard_map/ppermute | solution.py:365
  2.1 9.4 %collective-permute-start = (f32[6,16,128]{2,1,0:T(8,128)S(1)}, f32[6,16,128]{2,1,0:T(8,128)S(1)}, u32[]{:S(2)}, u32[]{:S(2)}) collective-permute-start(f32[6,16,128]{2,1,0:T(8,128)S(1)} %get-tuple-element.16.both), channel_id=1, source_target_pairs={{0,1},{1,0},{2,3},{3,2},{4,5},{5,4},{6,7},{7,6},{8,9},{9,8},{10,11... | collective-permute-start | bytes 147464 | tf_op jit(solution)/shard_map/ppermute | solution.py:366
  16.7 6.6 %collective-permute-start.3 = (f32[3,16,128]{2,1,0:T(8,128)S(1)}, f32[3,16,128]{2,1,0:T(8,128)S(1)}, u32[]{:S(2)}, u32[]{:S(2)}) collective-permute-start(f32[3,16,128]{2,1,0:T(8,128)S(1)} %get-tuple-element.22.vector.image), channel_id=1, source_target_pairs={{1,2},{2,1},{3,4},{4,3},{5,6},{6,5},{7,8},{8,7},{9,10},{10,9},{11,... | collective-permute-start | bytes 73736 | tf_op jit(solution)/shard_map/ppermute | solution.py:379
  17.6 5.8 %collective-permute-start.2 = (f32[3,16,128]{2,1,0:T(8,128)S(1)}, f32[3,16,128]{2,1,0:T(8,128)S(1)}, u32[]{:S(2)}, u32[]{:S(2)}) collective-permute-start(f32[3,16,128]{2,1,0:T(8,128)S(1)} %get-tuple-element.22.vector.image), channel_id=1, source_target_pairs={{0,1},{1,0},{2,3},{3,2},{4,5},{5,4},{6,7},{7,6},{8,9},{9,8},{10,11... | collective-permute-start | bytes 73736 | tf_op jit(solution)/shard_map/ppermute | solution.py:380

commit v4 on v3

--- a/solution.py
+++ b/solution.py
@@ -94,13 +94,17 @@
     return jnp.broadcast_to((1.0 - found) * DEAD, (FEATS, 128))
 
 
-def fold(acc, n):
-    both = acc[:, :128] + acc[:, 128:]
-    return (both[:n] + both[n : 2 * n] + both[2 * n :]) * (1.0 / 128)
-
-
 def beside(a, b):
     return jnp.concatenate([a, b], axis=1)
+
+
+def fold(high, low):
+    n = low.shape[0]
+    return (high[:n] + high[n : 2 * n] + high[2 * n :] + low) * (1.0 / 128)
+
+
+def pair_features(feats, k):
+    return beside(feats[2 * k], feats[2 * k + 1])
 
 
 def first_product(weights_ref, far_side, own_side, feats, put, pairs, window):
@@ -117,6 +121,7 @@
         push_own(0)
         for p in range(pairs):
             start = p if window else 0
+            high, low = outs[2 * (p % 2)], outs[2 * (p % 2) + 1]
             for t in range(pairs):
                 parts = [[], []]
                 for cc in range(2):
@@ -130,40 +135,46 @@
                     w = r * r
                     hi = w.astype(BF16)
                     lo = (w - hi.astype(F32)).astype(BF16)
-                    rows = slice(128 * cc, 128 * cc + 128)
-                    for q in range(2):
-                        cut = slice(128 * q, 128 * q + 128)
-                        weights_ref[2 * p + q, t, 0, rows] = hi[:, cut]
-                        weights_ref[2 * p + q, t, 1, rows] = lo[:, cut]
-                        parts[q].append(beside(hi[:, cut], lo[:, cut]))
-                f = beside(feats[2 * (start + t)], feats[2 * (start + t) + 1])
+                    rows = slice(8 * cc, 8 * cc + 8)
+                    for k, part in enumerate((hi, lo)):
+                        parts[k].append(part)
+                        for q in range(2):
+                            cut = slice(128 * q, 128 * q + 128)
+                            weights_ref[p, t, rows, 2 * k + q] = part[:, cut].reshape(8, 16, 128)
+                f = pair_features(feats, start + t)
+                for k, (acc, rows) in enumerate(((high, 3 * FEATS), (low, FEATS))):
+                    pltpu.matmul_push_rhs(jnp.concatenate(parts[k], axis=0), staging_register=k, mxu_index=1)
+                    pltpu.matmul_acc_lhs(acc, f[:rows], load_staged_rhs=k)
+            value = fold(pltpu.matmul_pop(high), pltpu.matmul_pop(low))
+            for q in range(2):
+                put(2 * p + q, value[:, 128 * q : 128 * q + 128])
+
+    soft = [pltpu.ACC(0)((128, 256), F32) for _ in range(depth)]
+    outs = [pltpu.ACC(1)((n, 256), F32) for n in (3 * FEATS, FEATS) * 2]
+    pl.run_scoped(body, *soft, *outs)
+
+
+def second_product(weights_ref, feats, put, pairs, window):
+    half = FEATS // 2
+
+    def body(*accs):
+        for first in range(0, pairs, 2):
+            turn = accs[4 * (first // 2 % 2) : 4 * (first // 2 % 2) + 4]
+            for t in range(pairs):
                 for q in range(2):
-                    pltpu.matmul_push_rhs(jnp.concatenate(parts[q], axis=0), staging_register=q, mxu_index=1)
-                    pltpu.matmul_acc_lhs(outs[2 * (p % 2) + q], f, load_staged_rhs=q)
+                    p = first + q
+                    f = pair_features(feats, (p if window else 0) + t)
+                    for k, rows in enumerate((3 * half, half)):
+                        tile = beside(*[weights_ref[p, t, :, 2 * k + i].reshape(256, 128) for i in range(2)])
+                        pltpu.matmul_push_rhs(tile, staging_register=k, mxu_index=q)
+                        pltpu.matmul_acc_lhs(turn[2 * q + k], f[:rows], load_staged_rhs=k)
             for q in range(2):
-                put(2 * p + q, fold(pltpu.matmul_pop(outs[2 * (p % 2) + q]), FEATS))
-
-    soft = [pltpu.ACC(0)((128, 256), F32) for _ in range(depth)]
-    outs = [pltpu.ACC(1)((3 * FEATS, 256), F32) for _ in range(4)]
-    pl.run_scoped(body, *soft, *outs)
-
-
-def second_product(weights_ref, feats, put, pairs, window):
-    rows = 3 * FEATS // 2
-
-    def body(*accs):
-        for p in range(pairs):
-            start = p if window else 0
-            for t in range(pairs):
-                f = beside(feats[2 * (start + t)], feats[2 * (start + t) + 1])
-                for q in range(2):
-                    tile = beside(weights_ref[2 * p + q, t, 0], weights_ref[2 * p + q, t, 1])
-                    pltpu.matmul_push_rhs(tile, staging_register=t % 2, mxu_index=q)
-                    pltpu.matmul_acc_lhs(accs[2 * q + p % 2], f, load_staged_rhs=t % 2)
-            for q in range(2):
-                put(2 * p + q, fold(pltpu.matmul_pop(accs[2 * q + p % 2]), FEATS // 2))
-
-    pl.run_scoped(body, *[pltpu.ACC(q)((rows, 256), F32) for q in (0, 0, 1, 1)])
+                value = fold(pltpu.matmul_pop(turn[2 * q]), pltpu.matmul_pop(turn[2 * q + 1]))
+                for i in range(2):
+                    put(2 * (first + q) + i, value[:, 128 * i : 128 * i + 128])
+
+    accs = [pltpu.ACC(q)((n, 256), F32) for _ in range(2) for q in range(2) for n in (3 * half, half)]
+    pl.run_scoped(body, *accs)
 
 
 def apply_local(field, feld_self, xs, vs, stiff, residual_rows):
@@ -351,7 +362,7 @@
     flip = lambda x: jnp.transpose(x, (1, 0, 2))
     vec = ((parts, blocks, atoms), F32)
     pair = ((2 * parts, blocks, atoms), F32)
-    wshape = ((blocks, blocks // 2, 2, 2 * atoms, atoms), BF16)
+    wshape = ((blocks // 2, blocks // 2, 2 * atoms // 16, 4, 16, atoms), BF16)
     own_scratch = ((blocks, 2 * FEATS, atoms), BF16)
     far = blocks * 2 - 2
 

time: 39.7 us -> 39.2 us (0.987)
  Pallas kernels: 17.7 us -> 17.2 us
    pallas_call x6, Pallas kernels: 17.7 us -> 17.2 us  [call(): pl.pallas_call(kernel, out_shape=[jax.ShapeDtypeStruct(s, d) for s, d in...]
where the time goes in v4:
time: 39.2 us; the launch traced here: 38.9 us
  Pallas kernels  17.2 us (44%)
  blocking collectives  12 us (31%)
  starting transfers between devices  8.81 us (22%)
  between operations  0.85 us (2%)
    pallas_call x6, Pallas kernels, call(): pl.pallas_call(kernel, out_shape=[jax.ShapeDtypeStruct(s, d) for s, d in...  17.2 us
    all_to_all x1, blocking collectives, per_device(): table = lax.all_to_all(sums, 'space', 0, 0, tiled=True)  12 us
    ppermute x1, starting transfers between devices, per_device(): mate = lax.ppermute(both, 'space', mates)  4.39 us
    ppermute x1, starting transfers between devices, per_device(): vmate = lax.ppermute(image, 'space', mates)  2.92 us
    ppermute x1, starting transfers between devices, per_device(): vother = lax.ppermute(image, 'space', others)  0.84 us
  transfers between devices with their start and end apart: 4, of which 0 were waited for; matrix products, arithmetic and copies ran while one was open for 0% of the time, Pallas kernels for 20%

profile of v4, /device:TPU:0, one launch (start us, length us, event | category | flops | bytes accessed | tf_op | source)
XLA Modules:
  0.0 38.9 jit_solution(10220530353917535572)
XLA Ops:
  0.6 0.8 %shard_map.68 = (f32[6,16,128]{2,1,0:T(8,128)S(1)}, f32[16,128]{1,0:T(8,128)S(1)}, s32[16,32]{1,0:T(8,128)S(1)}, s32[16,32]{1,0:T(8,128)S(1)}) custom-call(f32[3,16,128]{2,1,0:T(8,128)} %bitcast.10, f32[3,16,128]{2,1,0:T(8,128)} %bitcast.11, f32[16,128]{1,0:T(8,128)} %stiff.1, s32[16,32]{1,0:T(8,128)} %near.1, s32[16,32]{1,0:T(8,128)} %mask.1), custom_call_target="tpu_custom_call" | custom-call | tf_op jit(solution)/shard_map/pallas_call | solution.py:347
  1.4 0.7 %collective-permute-start.1 = (f32[6,16,128]{2,1,0:T(8,128)S(1)}, f32[6,16,128]{2,1,0:T(8,128)S(1)}, u32[]{:S(2)}, u32[]{:S(2)}) collective-permute-start(f32[6,16,128]{2,1,0:T(8,128)S(1)} %get-tuple-element.16.both), channel_id=1, source_target_pairs={{1,2},{2,1},{3,4},{4,3},{5,6},{6,5},{7,8},{8,7},{9,10},{10,9},{11,... | collective-permute-start | bytes 147464 | tf_op jit(solution)/shard_map/ppermute | solution.py:376
  2.1 4.4 %collective-permute-start = (f32[6,16,128]{2,1,0:T(8,128)S(1)}, f32[6,16,128]{2,1,0:T(8,128)S(1)}, u32[]{:S(2)}, u32[]{:S(2)}) collective-permute-start(f32[6,16,128]{2,1,0:T(8,128)S(1)} %get-tuple-element.16.both), channel_id=1, source_target_pairs={{0,1},{1,0},{2,3},{3,2},{4,5},{5,4},{6,7},{7,6},{8,9},{9,8},{10,11... | collective-permute-start | bytes 147464 | tf_op jit(solution)/shard_map/ppermute | solution.py:377
  6.5 5.1 %shard_map.69 = (bf16[8,8,16,4,16,128]{5,4,3,2,1,0:T(8,128)(2,1)S(1)}, f32[16,32,128]{2,1,0:T(8,128)S(1)}, f32[24,128]{1,0:T(8,128)S(1)}) custom-call(f32[6,16,128]{2,1,0:T(8,128)S(1)} %get-tuple-element.16.both, s32[16,32]{1,0:T(8,128)S(1)} %get-tuple-element.18.near, s32[16,32]{1,0:T(8,128)S(1)} %get-tuple-element.19.mask), custom_call_target="tpu_custom_call" | custom-call | tf_op jit(solution)/shard_map/pallas_call | solution.py:347
  11.6 0.0 collective-permute-done.1.other
  11.6 0.0 collective-permute-done.mate
  11.6 5.1 %shard_map.70 = (bf16[8,8,16,4,16,128]{5,4,3,2,1,0:T(8,128)(2,1)S(1)}, f32[16,16,128]{2,1,0:T(8,128)S(1)}, f32[3,16,128]{2,1,0:T(8,128)S(1)}) custom-call(f32[6,16,128]{2,1,0:T(8,128)S(1)} %collective-permute-done.mate, f32[6,16,128]{2,1,0:T(8,128)S(1)} %collective-permute-done.1.other, f32[6,16,128]{2,1,0:T(8,128)S(1)} %get-tuple-element.16.both, ...), custom_call_target="tpu_custom_call" | custom-call | tf_op jit(solution)/shard_map/pallas_call | solution.py:347
  16.8 0.8 %collective-permute-start.3 = (f32[3,16,128]{2,1,0:T(8,128)S(1)}, f32[3,16,128]{2,1,0:T(8,128)S(1)}, u32[]{:S(2)}, u32[]{:S(2)}) collective-permute-start(f32[3,16,128]{2,1,0:T(8,128)S(1)} %get-tuple-element.22.vector.image), channel_id=1, source_target_pairs={{1,2},{2,1},{3,4},{4,3},{5,6},{6,5},{7,8},{8,7},{9,10},{10,9},{11,... | collective-permute-start | bytes 73736 | tf_op jit(solution)/shard_map/ppermute | solution.py:390
  17.6 2.9 %collective-permute-start.2 = (f32[3,16,128]{2,1,0:T(8,128)S(1)}, f32[3,16,128]{2,1,0:T(8,128)S(1)}, u32[]{:S(2)}, u32[]{:S(2)}) collective-permute-start(f32[3,16,128]{2,1,0:T(8,128)S(1)} %get-tuple-element.22.vector.image), channel_id=1, source_target_pairs={{0,1},{1,0},{2,3},{3,2},{4,5},{5,4},{6,7},{7,6},{8,9},{9,8},{10,11... | collective-permute-start | bytes 73736 | tf_op jit(solution)/shard_map/ppermute | solution.py:391
  20.5 2.6 %shard_map.71.field_in = f32[16,16,128]{2,1,0:T(8,128)S(1)} custom-call(f32[6,16,128]{2,1,0:T(8,128)S(1)} %get-tuple-element.16.both, f32[3,16,128]{2,1,0:T(8,128)S(1)} %get-tuple-element.22.vector.image, f32[24,128]{1,0:T(8,128)S(1)} %get-tuple-element.20.centre_in, bf16[8,8,16,4,16,128]{5,4,3,2,1,0:T(8,128)(2,1)S(1)} %get-tuple-element.24.weights), custom_call_target="tpu_custom_call" | custom-call | tf_op jit(solution)/shard_map/pallas_call | solution.py:347
  23.1 0.0 collective-permute-done.3.vother
  23.1 0.0 collective-permute-done.2.vmate
  23.1 2.8 %shard_map.72 = (f32[3,16,128]{2,1,0:T(8,128)S(1)}, f32[32,128]{1,0:T(8,128)S(1)}) custom-call(f32[3,16,128]{2,1,0:T(8,128)S(1)} %collective-permute-done.2.vmate, f32[3,16,128]{2,1,0:T(8,128)S(1)} %collective-permute-done.3.vother, f32[6,16,128]{2,1,0:T(8,128)S(1)} %collective-permute-done.mate, f32[6,16,128]{2,1,0:T(8,128)S(1)} %collective-permute-done.1.other, ...), custom_call_target="tpu_custom_call" | custom-call | tf_op jit(solution)/shard_map/pallas_call | solution.py:347
  26.0 12.0 %all_to_all.11 = f32[32,1,128]{2,1,0:T(1,128)S(1)} all-to-all(f32[32,1,128]{2,1,0:T(1,128)S(1)} %bitcast.9), channel_id=1, replica_groups=mesh['space'=32] {'space'}, dimensions={0} | all-to-all | bytes 32768 | tf_op jit(solution)/shard_map/all_to_all | solution.py:404
  38.0 0.8 %shard_map.73 = (f32[3,16,128]{2,1,0:T(8,128)}, f32[3,16,128]{2,1,0:T(8,128)}) custom-call(f32[32,128]{1,0:T(8,128)S(1)} %bitcast.8, f32[6,16,128]{2,1,0:T(8,128)S(1)} %get-tuple-element.16.both, f32[3,16,128]{2,1,0:T(8,128)S(1)} %get-tuple-element.22.vector.image, f32[3,16,128]{2,1,0:T(8,128)S(1)} %get-tuple-element.27.image2), custom_call_target="tpu_custom_call" | custom-call | tf_op jit(solution)/shard_map/pallas_call | solution.py:347
Async XLA Ops:
  1.4 10.2 %collective-permute-start.1 = (f32[6,16,128]{2,1,0:T(8,128)S(1)}, f32[6,16,128]{2,1,0:T(8,128)S(1)}, u32[]{:S(2)}, u32[]{:S(2)}) collective-permute-start(f32[6,16,128]{2,1,0:T(8,128)S(1)} %get-tuple-element.16.both), channel_id=1, source_target_pairs={{1,2},{2,1},{3,4},{4,3},{5,6},{6,5},{7,8},{8,7},{9,10},{10,9},{11,... | collective-permute-start | bytes 147464 | tf_op jit(solution)/shard_map/ppermute | solution.py:376
  2.1 9.5 %collective-permute-start = (f32[6,16,128]{2,1,0:T(8,128)S(1)}, f32[6,16,128]{2,1,0:T(8,128)S(1)}, u32[]{:S(2)}, u32[]{:S(2)}) collective-permute-start(f32[6,16,128]{2,1,0:T(8,128)S(1)} %get-tuple-element.16.both), channel_id=1, source_target_pairs={{0,1},{1,0},{2,3},{3,2},{4,5},{5,4},{6,7},{7,6},{8,9},{9,8},{10,11... | collective-permute-start | bytes 147464 | tf_op jit(solution)/shard_map/ppermute | solution.py:377
  16.8 6.4 %collective-permute-start.3 = (f32[3,16,128]{2,1,0:T(8,128)S(1)}, f32[3,16,128]{2,1,0:T(8,128)S(1)}, u32[]{:S(2)}, u32[]{:S(2)}) collective-permute-start(f32[3,16,128]{2,1,0:T(8,128)S(1)} %get-tuple-element.22.vector.image), channel_id=1, source_target_pairs={{1,2},{2,1},{3,4},{4,3},{5,6},{6,5},{7,8},{8,7},{9,10},{10,9},{11,... | collective-permute-start | bytes 73736 | tf_op jit(solution)/shard_map/ppermute | solution.py:390
  17.6 5.5 %collective-permute-start.2 = (f32[3,16,128]{2,1,0:T(8,128)S(1)}, f32[3,16,128]{2,1,0:T(8,128)S(1)}, u32[]{:S(2)}, u32[]{:S(2)}) collective-permute-start(f32[3,16,128]{2,1,0:T(8,128)S(1)} %get-tuple-element.22.vector.image), channel_id=1, source_target_pairs={{0,1},{1,0},{2,3},{3,2},{4,5},{5,4},{6,7},{7,6},{8,9},{9,8},{10,11... | collective-permute-start | bytes 73736 | tf_op jit(solution)/shard_map/ppermute | solution.py:391
